TPU v7x, 256 devices: a whole 4x4x8 slice. The times are simulated.
256 devices in a mesh: gz: 256 (over y, z, x, core).
Axes of the slice: x: 4, y: 4, z: 8, core: 2. Of those that a mesh axis runs over, the one named last changes fastest.
Arguments:
- state: float32 [8, 256, 64, 256], P(None, 'gz'), may hold values from -18 to 18
- explicit_rhs: float32 [2, 8, 256, 64, 256], P(None, None, 'gz'), may hold values from -6 to 6
- implicit_rhs: float32 [2, 8, 256, 64, 256], P(None, None, 'gz'), may hold values from -6 to 6
- implicit_coef: float32 [8], replicated, may hold values from 0.5 to 4
Outputs:
- section_value: float32 [8, 256, 64, 256], P(None, 'gz')
- weighted_rms: float32 [], replicated
All inputs are finite; a program needn't handle non-finite values.
Results may differ from a plain program's by a relative error of at most 0.0001.
Values sent between devices are 32-bit elements; how exact they have to be, the bound alone decides.
A program may use at most 64 MiB of HBM per device.

v0:
```python
import jax
import jax.numpy as jnp
from jax import lax
from jax.sharding import Mesh
from jax.sharding import PartitionSpec as P

ITERS = 3
GZ = ("gz_0", "gz_1", "gz_2", "gz_3")


explicit_weights = (5535828885825.0 / 10492691773637.0, 788022342437.0 / 10882634858940.0)
implicit_weights = (2746238789719.0 / 10658868560708.0, -640167445237.0 / 6845629431997.0)


def extended(block, sides, width):
    for axis, dim in sides:
        count = lax.axis_size(axis)
        forward = [(i, i + 1) for i in range(count - 1)]
        forward.append((count - 1, 0))
        backward = [(target, source) for source, target in forward]
        low = lax.ppermute(
            lax.slice_in_dim(block, block.shape[dim] - width, None, axis=dim), axis, forward
        )
        high = lax.ppermute(lax.slice_in_dim(block, 0, width, axis=dim), axis, backward)
        block = jnp.concatenate([low, block, high], axis=dim)
    return block


def copy_for_each(value, axis):
    copies = jnp.broadcast_to(value, (lax.axis_size(axis), *value.shape))
    return lax.all_to_all(copies, axis, split_axis=0, concat_axis=0, tiled=True)


def over_copies(value, axis):
    return copy_for_each(value, axis).sum(axis=0)


def over_axes(value, axes):
    far, near = axes
    nearer = over_copies(value, near)
    return over_copies(nearer, far)


def together(arrays, axis):
    ravelled, at, done = (jnp.concatenate([a.reshape(-1) for a in arrays]), 0, [])
    total = over_axes(ravelled, axis)
    for a in arrays:
        done.append(total[at : at + a.size].reshape(a.shape))
        at += a.size
    return tuple(done)


def operate(field, implicit_coef):
    padded = extended(field, ((GZ, 1),), 1)
    flat = jnp.pad(field, ((0, 0), (0, 0), (1, 1), (1, 1)))
    beside = padded[:, 2:] + padded[:, :-2]
    beside = (
        beside
        + flat[:, :, 2:, 1:-1]
        + flat[:, :, :-2, 1:-1]
        + flat[:, :, 1:-1, 2:]
        + flat[:, :, 1:-1, :-2]
    )
    return field - implicit_coef[:, None, None, None] * (beside - 6.0 * field)


def species_sum(first, second):
    return jnp.sum(first * second, axis=(1, 2, 3))


def widen(values):
    return values[:, None, None, None]


def paired_totals(residual, image):
    return together(
        (species_sum(residual, residual), species_sum(residual, image)),
        (("gz_0", "gz_1"), ("gz_2", "gz_3")),
    )


def shards(state, explicit_rhs, implicit_rhs, implicit_coef):
    section_in = (
        state + explicit_weights[0] * explicit_rhs[0] + explicit_weights[1] * explicit_rhs[1]
    )
    section_in = (
        section_in + implicit_weights[0] * implicit_rhs[0] + implicit_weights[1] * implicit_rhs[1]
    )
    solution = section_in
    residual = section_in - operate(section_in, implicit_coef)
    image = operate(residual, implicit_coef)
    norm_now, product = paired_totals(residual, image)
    step_size = norm_now / product
    direction, along = (residual, image)
    for iteration in range(ITERS):
        solution = solution + widen(step_size) * direction
        residual = residual - widen(step_size) * along
        if iteration + 1 < ITERS:
            image = operate(residual, implicit_coef)
            norm_next, product = paired_totals(residual, image)
            beta_ratio = norm_next / norm_now
            step_size = norm_next / (product - beta_ratio * norm_next / step_size)
            direction = residual + widen(beta_ratio) * direction
            along = image + widen(beta_ratio) * along
            norm_now = norm_next
    scaled = (solution - section_in) / (1.0 + 0.1 * jnp.abs(state))
    summed = over_axes(jnp.sum(scaled * scaled), (("gz_0", "gz_1"), ("gz_2", "gz_3")))
    cells = state.shape[0] * state.shape[1] * state.shape[2] * state.shape[3] * lax.axis_size(GZ)
    weighted_rms = jnp.sqrt(summed / cells)
    return (solution, weighted_rms)


def solution(mesh):
    torus = Mesh(mesh.devices.reshape(4, 8, 4, 2), ("gz_0", "gz_1", "gz_2", "gz_3"))
    placed = (
        P(None, GZ, None, None),
        P(None, None, GZ, None, None),
        P(None, None, GZ, None, None),
        P(),
    )
    return jax.shard_map(
        shards,
        mesh=torus,
        in_specs=placed,
        out_specs=(P(None, GZ, None, None), P()),
        check_vma=False,
    )
```

profile of v0, /device:TPU:1, one launch (start us, length us, event | category | flops | bytes accessed | tf_op | source)
XLA Modules:
  0.0 167.4 jit_solution(9812153086053562143)
XLA Ops:
  0.6 0.0 copy-start.1
  0.6 1.9 %fusion.28 = f32[8,1,64,256]{3,2,1,0:T(8,128)S(1)} fusion(f32[2,8,1,64,256]{4,3,1,2,0:T(8,128)} %bitcast.27, f32[2,8,1,64,256]{4,3,1,2,0:T(8,128)} %bitcast.28, f32[8,1,64,256]{3,2,1,0:T(8,128)} %param.4), kind=kLoop, calls=%fused_computation.47 | loop fusion | flops 1048576 | bytes 3145728 | tf_op jit(solution)/shard_map/add | solution.py:87
  2.5 2.7 %collective-permute-start.1 = (f32[8,1,64,256]{3,2,1,0:T(8,128)S(1)}, f32[8,1,64,256]{3,2,1,0:T(8,128)S(1)}, u32[]{:S(2)}, u32[]{:S(2)}) collective-permute-start(f32[8,1,64,256]{3,2,1,0:T(8,128)S(1)} %fusion.28), channel_id=1, source_target_pairs={{0,1},{1,2},{2,3},{3,4},{4,5},{5,6},{6,7},{7,8},{8,9},{9,10},{10,1... | collective-permute-start | bytes 1572872 | tf_op jit(solution)/shard_map/ppermute | solution.py:21
  5.2 0.7 collective-permute-start
  5.9 5.4 %collective-permute-done.1 = f32[8,1,64,256]{3,2,1,0:T(8,128)S(1)} collective-permute-done((f32[8,1,64,256]{3,2,1,0:T(8,128)S(1)}, f32[8,1,64,256]{3,2,1,0:T(8,128)S(1)}, u32[]{:S(2)}, u32[]{:S(2)}) %collective-permute-start.1) | collective-permute-done | bytes 524320 | tf_op jit(solution)/shard_map/ppermute | solution.py:21
  11.3 2.5 %collective-permute-done = f32[8,1,64,256]{3,2,1,0:T(8,128)S(1)} collective-permute-done((f32[8,1,64,256]{3,2,1,0:T(8,128)S(1)}, f32[8,1,64,256]{3,2,1,0:T(8,128)S(1)}, u32[]{:S(2)}, u32[]{:S(2)}) %collective-permute-start) | collective-permute-done | bytes 524320 | tf_op jit(solution)/shard_map/ppermute | solution.py:24
  13.8 0.0 copy-done.1
  13.8 0.4 subtract_subtract_fusion
  14.2 0.1 collective-permute-start.3
  14.3 7.2 %collective-permute-start.2 = (f32[8,1,64,256]{3,2,1,0:T(8,128)S(1)}, f32[8,1,64,256]{3,2,1,0:T(8,128)S(1)}, u32[]{:S(2)}, u32[]{:S(2)}) collective-permute-start(f32[8,1,64,256]{3,2,1,0:T(8,128)S(1)} %subtract_subtract_fusion), channel_id=1, source_target_pairs={{1,0},{2,1},{3,2},{4,3},{5,4},{6,5},{7,6},{8,7},{9,8},{10,9},{11,1... | collective-permute-start | bytes 1572872 | tf_op jit(solution)/shard_map/ppermute | solution.py:24
  21.5 1.3 collective-permute-done.3
  22.8 0.2 collective-permute-done.2
  23.0 0.5 multiply_reduce_fusion.5
  23.6 0.1 pad_maximum_fusion
  23.7 19.4 %all_to_all.48 = f32[8,1,16]{2,1,0:T(1,128)S(1)} all-to-all(f32[8,1,16]{2,1,0:T(1,128)S(1)} %broadcast_in_dim.16), channel_id=1, replica_groups=mesh['gz_0'=4,'gz_1'=8,'gz_2'=4,'gz_3'=2] {'gz_2','gz_3'}, dimensions={0} | all-to-all | bytes 1024 | tf_op jit(solution)/shard_map/all_to_all | solution.py:31
  43.1 16.4 %all_to_all.49 = f32[32,1,16]{2,1,0:T(1,128)S(1)} all-to-all(f32[32,1,16]{2,1,0:T(1,128)S(1)} %broadcast_in_dim.17), channel_id=1, replica_groups=mesh['gz_0'=4,'gz_1'=8,'gz_2'=4,'gz_3'=2] {'gz_0','gz_1'}, dimensions={0} | all-to-all | bytes 4096 | tf_op jit(solution)/shard_map/all_to_all | solution.py:31
  59.5 0.1 reduce_sum.138
  59.6 0.1 slice_divide_fusion.1
  59.6 0.1 multiply_subtract_fusion.1
  59.8 2.4 %collective-permute-start.5 = (f32[8,1,64,256]{3,2,1,0:T(8,128)S(1)}, f32[8,1,64,256]{3,2,1,0:T(8,128)S(1)}, u32[]{:S(2)}, u32[]{:S(2)}) collective-permute-start(f32[8,1,64,256]{3,2,1,0:T(8,128)S(1)} %multiply_subtract_fusion.1), channel_id=1, source_target_pairs={{0,1},{1,2},{2,3},{3,4},{4,5},{5,6},{6,7},{7,8},{8,9},{9,10},{10,1... | collective-permute-start | bytes 1572872 | tf_op jit(solution)/shard_map/ppermute | solution.py:21
  62.1 0.0 collective-permute-start.4
  62.1 6.1 %collective-permute-done.5 = f32[8,1,64,256]{3,2,1,0:T(8,128)S(1)} collective-permute-done((f32[8,1,64,256]{3,2,1,0:T(8,128)S(1)}, f32[8,1,64,256]{3,2,1,0:T(8,128)S(1)}, u32[]{:S(2)}, u32[]{:S(2)}) %collective-permute-start.5) | collective-permute-done | bytes 524320 | tf_op jit(solution)/shard_map/ppermute | solution.py:21
  68.3 2.8 %collective-permute-done.4 = f32[8,1,64,256]{3,2,1,0:T(8,128)S(1)} collective-permute-done((f32[8,1,64,256]{3,2,1,0:T(8,128)S(1)}, f32[8,1,64,256]{3,2,1,0:T(8,128)S(1)}, u32[]{:S(2)}, u32[]{:S(2)}) %collective-permute-start.4) | collective-permute-done | bytes 524320 | tf_op jit(solution)/shard_map/ppermute | solution.py:24
  71.0 0.6 multiply_reduce_fusion.3
  71.6 0.1 pad_maximum_fusion.1
  71.7 11.9 %all_to_all.50 = f32[8,1,16]{2,1,0:T(1,128)S(1)} all-to-all(f32[8,1,16]{2,1,0:T(1,128)S(1)} %broadcast_in_dim.18), channel_id=1, replica_groups=mesh['gz_0'=4,'gz_1'=8,'gz_2'=4,'gz_3'=2] {'gz_2','gz_3'}, dimensions={0} | all-to-all | bytes 1024 | tf_op jit(solution)/shard_map/all_to_all | solution.py:31
  83.6 16.3 %all_to_all.51 = f32[32,1,16]{2,1,0:T(1,128)S(1)} all-to-all(f32[32,1,16]{2,1,0:T(1,128)S(1)} %broadcast_in_dim.19), channel_id=1, replica_groups=mesh['gz_0'=4,'gz_1'=8,'gz_2'=4,'gz_3'=2] {'gz_0','gz_1'}, dimensions={0} | all-to-all | bytes 4096 | tf_op jit(solution)/shard_map/all_to_all | solution.py:31
  99.9 0.1 reduce_sum.142
  100.0 0.1 slice_divide_fusion.3
  100.1 0.2 multiply_subtract_fusion
  100.2 0.0 copy-start
  100.2 2.4 %collective-permute-start.7 = (f32[8,1,64,256]{3,2,1,0:T(8,128)S(1)}, f32[8,1,64,256]{3,2,1,0:T(8,128)S(1)}, u32[]{:S(2)}, u32[]{:S(2)}) collective-permute-start(f32[8,1,64,256]{3,2,1,0:T(8,128)S(1)} %multiply_subtract_fusion), channel_id=1, source_target_pairs={{0,1},{1,2},{2,3},{3,4},{4,5},{5,6},{6,7},{7,8},{8,9},{9,10},{10,1... | collective-permute-start | bytes 1572872 | tf_op jit(solution)/shard_map/ppermute | solution.py:21
  102.6 0.0 collective-permute-start.6
  102.6 6.1 %collective-permute-done.7 = f32[8,1,64,256]{3,2,1,0:T(8,128)S(1)} collective-permute-done((f32[8,1,64,256]{3,2,1,0:T(8,128)S(1)}, f32[8,1,64,256]{3,2,1,0:T(8,128)S(1)}, u32[]{:S(2)}, u32[]{:S(2)}) %collective-permute-start.7) | collective-permute-done | bytes 524320 | tf_op jit(solution)/shard_map/ppermute | solution.py:21
  108.7 2.8 %collective-permute-done.6 = f32[8,1,64,256]{3,2,1,0:T(8,128)S(1)} collective-permute-done((f32[8,1,64,256]{3,2,1,0:T(8,128)S(1)}, f32[8,1,64,256]{3,2,1,0:T(8,128)S(1)}, u32[]{:S(2)}, u32[]{:S(2)}) %collective-permute-start.6) | collective-permute-done | bytes 524320 | tf_op jit(solution)/shard_map/ppermute | solution.py:24
  111.5 0.6 multiply_reduce_fusion.1
  112.1 0.1 pad_maximum_fusion.2
  112.2 11.9 %all_to_all.52 = f32[8,1,16]{2,1,0:T(1,128)S(1)} all-to-all(f32[8,1,16]{2,1,0:T(1,128)S(1)} %broadcast_in_dim.40), channel_id=1, replica_groups=mesh['gz_0'=4,'gz_1'=8,'gz_2'=4,'gz_3'=2] {'gz_2','gz_3'}, dimensions={0} | all-to-all | bytes 1024 | tf_op jit(solution)/shard_map/all_to_all | solution.py:31
  124.1 16.3 %all_to_all.53 = f32[32,1,16]{2,1,0:T(1,128)S(1)} all-to-all(f32[32,1,16]{2,1,0:T(1,128)S(1)} %broadcast_in_dim.41), channel_id=1, replica_groups=mesh['gz_0'=4,'gz_1'=8,'gz_2'=4,'gz_3'=2] {'gz_0','gz_1'}, dimensions={0} | all-to-all | bytes 4096 | tf_op jit(solution)/shard_map/all_to_all | solution.py:31
  140.4 0.1 reduce_sum.146
  140.5 0.1 subtract_divide_fusion
  140.6 1.7 %multiply_reduce_fusion = (f32[]{:T(128)}, f32[8,1,64,256]{3,2,1,0:T(8,128)}) fusion(f32[8,1,64,256]{3,2,1,0:T(8,128)S(1)} %copy-done, f32[8,1,64,256]{3,2,1,0:T(8,128)S(1)} %fusion.28, f32[8,1,64,256]{3,2,1,0:T(8,128)S(1)} %multiply_subtract_fusion, f32[8]{0:T(128)S(1)} %get-tuple-element.11, f32[8]{0:T(128)S(1)} %get-tuple-element.10, ...), kind=kLoop, calls=%fused_computation.57 | loop fusion | flops 2228223 | bytes 3145892 | tf_op jit(solution)/shard_map/reduce_sum | solution.py:107
  142.3 0.6 broadcast_in_dim.42
  142.9 9.1 %all_to_all.54 = f32[8,1,1]{2,1,0:T(1,128)S(1)} all-to-all(f32[8,1,1]{2,1,0:T(1,128)S(1)} %broadcast_in_dim.42), channel_id=1, replica_groups=mesh['gz_0'=4,'gz_1'=8,'gz_2'=4,'gz_3'=2] {'gz_2','gz_3'}, dimensions={0} | all-to-all | bytes 64 | tf_op jit(solution)/shard_map/all_to_all | solution.py:31
  152.0 0.6 reduce_sum.148
  152.6 0.7 broadcast_in_dim.43
  153.3 11.6 %all_to_all.55 = f32[32,1,1]{2,1,0:T(1,128)S(1)} all-to-all(f32[32,1,1]{2,1,0:T(1,128)S(1)} %broadcast_in_dim.43), channel_id=1, replica_groups=mesh['gz_0'=4,'gz_1'=8,'gz_2'=4,'gz_3'=2] {'gz_0','gz_1'}, dimensions={0} | all-to-all | bytes 256 | tf_op jit(solution)/shard_map/all_to_all | solution.py:31
  164.9 0.6 reduce_sum.149
  (10 shorter events, 0.1 us)
Async XLA Ops:
  0.6 13.2 %copy-start.1 = (f32[8]{0:T(128)S(1)}, f32[8]{0:T(128)}, u32[]{:S(2)}) copy-start(f32[8]{0:T(128)} %param.7) | copy-start | bytes 100
  2.5 8.8 %collective-permute-start.1 = (f32[8,1,64,256]{3,2,1,0:T(8,128)S(1)}, f32[8,1,64,256]{3,2,1,0:T(8,128)S(1)}, u32[]{:S(2)}, u32[]{:S(2)}) collective-permute-start(f32[8,1,64,256]{3,2,1,0:T(8,128)S(1)} %fusion.28), channel_id=1, source_target_pairs={{0,1},{1,2},{2,3},{3,4},{4,5},{5,6},{6,7},{7,8},{8,9},{9,10},{10,1... | collective-permute-start | bytes 1572872 | tf_op jit(solution)/shard_map/ppermute | solution.py:21
  5.2 8.6 %collective-permute-start = (f32[8,1,64,256]{3,2,1,0:T(8,128)S(1)}, f32[8,1,64,256]{3,2,1,0:T(8,128)S(1)}, u32[]{:S(2)}, u32[]{:S(2)}) collective-permute-start(f32[8,1,64,256]{3,2,1,0:T(8,128)S(1)} %fusion.28), channel_id=1, source_target_pairs={{1,0},{2,1},{3,2},{4,3},{5,4},{6,5},{7,6},{8,7},{9,8},{10,9},{11,1... | collective-permute-start | bytes 1572872 | tf_op jit(solution)/shard_map/ppermute | solution.py:24
  14.2 8.6 %collective-permute-start.3 = (f32[8,1,64,256]{3,2,1,0:T(8,128)S(1)}, f32[8,1,64,256]{3,2,1,0:T(8,128)S(1)}, u32[]{:S(2)}, u32[]{:S(2)}) collective-permute-start(f32[8,1,64,256]{3,2,1,0:T(8,128)S(1)} %subtract_subtract_fusion), channel_id=1, source_target_pairs={{0,1},{1,2},{2,3},{3,4},{4,5},{5,6},{6,7},{7,8},{8,9},{9,10},{10,1... | collective-permute-start | bytes 1572872 | tf_op jit(solution)/shard_map/ppermute | solution.py:21
  14.3 8.7 %collective-permute-start.2 = (f32[8,1,64,256]{3,2,1,0:T(8,128)S(1)}, f32[8,1,64,256]{3,2,1,0:T(8,128)S(1)}, u32[]{:S(2)}, u32[]{:S(2)}) collective-permute-start(f32[8,1,64,256]{3,2,1,0:T(8,128)S(1)} %subtract_subtract_fusion), channel_id=1, source_target_pairs={{1,0},{2,1},{3,2},{4,3},{5,4},{6,5},{7,6},{8,7},{9,8},{10,9},{11,1... | collective-permute-start | bytes 1572872 | tf_op jit(solution)/shard_map/ppermute | solution.py:24
  59.8 8.5 %collective-permute-start.5 = (f32[8,1,64,256]{3,2,1,0:T(8,128)S(1)}, f32[8,1,64,256]{3,2,1,0:T(8,128)S(1)}, u32[]{:S(2)}, u32[]{:S(2)}) collective-permute-start(f32[8,1,64,256]{3,2,1,0:T(8,128)S(1)} %multiply_subtract_fusion.1), channel_id=1, source_target_pairs={{0,1},{1,2},{2,3},{3,4},{4,5},{5,6},{6,7},{7,8},{8,9},{9,10},{10,1... | collective-permute-start | bytes 1572872 | tf_op jit(solution)/shard_map/ppermute | solution.py:21
  62.1 8.9 %collective-permute-start.4 = (f32[8,1,64,256]{3,2,1,0:T(8,128)S(1)}, f32[8,1,64,256]{3,2,1,0:T(8,128)S(1)}, u32[]{:S(2)}, u32[]{:S(2)}) collective-permute-start(f32[8,1,64,256]{3,2,1,0:T(8,128)S(1)} %multiply_subtract_fusion.1), channel_id=1, source_target_pairs={{1,0},{2,1},{3,2},{4,3},{5,4},{6,5},{7,6},{8,7},{9,8},{10,9},{11,1... | collective-permute-start | bytes 1572872 | tf_op jit(solution)/shard_map/ppermute | solution.py:24
  100.2 40.3 %copy-start = (f32[8,1,64,256]{3,2,1,0:T(8,128)S(1)}, f32[8,1,64,256]{3,2,1,0:T(8,128)}, u32[]{:S(2)}) copy-start(f32[8,1,64,256]{3,2,1,0:T(8,128)} %param.4) | copy-start | bytes 1572868
  100.2 8.5 %collective-permute-start.7 = (f32[8,1,64,256]{3,2,1,0:T(8,128)S(1)}, f32[8,1,64,256]{3,2,1,0:T(8,128)S(1)}, u32[]{:S(2)}, u32[]{:S(2)}) collective-permute-start(f32[8,1,64,256]{3,2,1,0:T(8,128)S(1)} %multiply_subtract_fusion), channel_id=1, source_target_pairs={{0,1},{1,2},{2,3},{3,4},{4,5},{5,6},{6,7},{7,8},{8,9},{9,10},{10,1... | collective-permute-start | bytes 1572872 | tf_op jit(solution)/shard_map/ppermute | solution.py:21
  102.6 8.9 %collective-permute-start.6 = (f32[8,1,64,256]{3,2,1,0:T(8,128)S(1)}, f32[8,1,64,256]{3,2,1,0:T(8,128)S(1)}, u32[]{:S(2)}, u32[]{:S(2)}) collective-permute-start(f32[8,1,64,256]{3,2,1,0:T(8,128)S(1)} %multiply_subtract_fusion), channel_id=1, source_target_pairs={{1,0},{2,1},{3,2},{4,3},{5,4},{6,5},{7,6},{8,7},{9,8},{10,9},{11,1... | collective-permute-start | bytes 1572872 | tf_op jit(solution)/shard_map/ppermute | solution.py:24
where the time goes:
time: 168 us; the launch traced here: 167 us
  blocking collectives  113 us (67%)
  waiting for transfers between devices  27.2 us (16%)
  starting transfers between devices  15.4 us (9%)
  other arithmetic  7.86 us (5%)
  between operations  2.54 us (2%)
    all_to_all x8, blocking collectives, copy_for_each(): return lax.all_to_all(copies, axis, split_axis=0, concat_axis=0, tiled=True)  113 us
    ppermute x4, waiting for transfers between devices, extended(): lax.ppermute(lax.slice_in_dim(block, block.shape[dim] - width, None, axis...  19 us
    ppermute x4, waiting for transfers between devices, extended(): lax.ppermute(lax.slice_in_dim(block, 0, width, axis=dim), axis, backward)  8.25 us
    ppermute x4, starting transfers between devices, extended(): lax.ppermute(lax.slice_in_dim(block, 0, width, axis=dim), axis, backward)  7.89 us
    ppermute x4, starting transfers between devices, extended(): lax.ppermute(lax.slice_in_dim(block, block.shape[dim] - width, None, axis...  7.49 us
  transfers between devices with their start and end apart: 8, of which 8 were waited for; matrix products, arithmetic and copies ran while one was open for 0% of the time, Pallas kernels for 0%

commit v1 on v0

v1 whole, which is shorter than its diff:
```python
import functools

import jax
import jax.numpy as jnp
from jax import lax
from jax.experimental import pallas as pl
from jax.experimental.pallas import tpu as pltpu
from jax.sharding import Mesh
from jax.sharding import PartitionSpec as P

AXES = ("gz_0", "gz_1", "gz_2", "gz_3")
MESH = pl.DeviceIdType.MESH

explicit_weights = (5535828885825.0 / 10492691773637.0, 788022342437.0 / 10882634858940.0)
implicit_weights = (2746238789719.0 / 10658868560708.0, -640167445237.0 / 6845629431997.0)

HALO = 4
RING = 8
MOMENTS = 6
SHIFT = 8.0


def remote(src, dst, send, recv, device):
    return pltpu.make_async_remote_copy(
        src_ref=src,
        dst_ref=dst,
        send_sem=send,
        recv_sem=recv,
        device_id=device,
        device_id_type=MESH,
    )


def laplace(below, here, above, shift=0.0):
    ny, nx = here.shape
    row = lax.broadcasted_iota(jnp.int32, here.shape, 0)
    lane = lax.broadcasted_iota(jnp.int32, here.shape, 1)
    beside = below + above
    beside = beside + jnp.where(row == ny - 1, 0.0, pltpu.roll(here, ny - 1, 0))
    beside = beside + jnp.where(row == 0, 0.0, pltpu.roll(here, 1, 0))
    beside = beside + jnp.where(lane == nx - 1, 0.0, pltpu.roll(here, nx - 1, 1))
    beside = beside + jnp.where(lane == 0, 0.0, pltpu.roll(here, 1, 1))
    return (6.0 - shift) * here - beside


def folded(value):
    total = value[0:8]
    for at in range(8, value.shape[0], 8):
        total = total + value[at : at + 8]
    return total


def row_of(sums):
    lane = lax.broadcasted_iota(jnp.int32, (1, 128), 1)
    row = jnp.zeros((1, 128), jnp.float32)
    for k, value in enumerate(sums):
        row = jnp.where(lane == k, jnp.sum(value, axis=(0, 1), keepdims=True), row)
    return row


def entries(row, count):
    lane = lax.broadcasted_iota(jnp.int32, (1, 128), 1)
    return [
        jnp.sum(jnp.where(lane == k, row, 0.0), axis=1, keepdims=True) for k in range(count)
    ]


def basis_steps(nu, c):
    diagonal = 1.0 + SHIFT * c

    def gram(p, shift):
        total = None
        for i, a in enumerate(p):
            for j, b in enumerate(p):
                term = a * b * nu[i + j + shift]
                total = term if total is None else total + term
        return total

    def step(norm, along):
        energy = jnp.maximum(diagonal * gram(along, 0) + c * gram(along, 1), norm)
        return jnp.where(norm > 0.0, norm / energy, 0.0)

    norm = nu[0]
    first = norm / (diagonal * nu[0] + c * nu[1])
    residual = (1.0 - first * diagonal, -first * c)
    norm_next = jnp.maximum(gram(residual, 0), 0.0)
    ratio = norm_next / norm
    along = (residual[0] + ratio, residual[1])
    second = step(norm_next, along)
    norm = norm_next
    image = (diagonal * along[0], diagonal * along[1] + c * along[0], c * along[1])
    residual = (
        residual[0] - second * image[0],
        residual[1] - second * image[1],
        -second * image[2],
    )
    norm_next = jnp.maximum(gram(residual, 0), 0.0)
    ratio = jnp.where(norm > 0.0, norm_next / norm, 0.0)
    last = (residual[0] + ratio * along[0], residual[1] + ratio * along[1], residual[2])
    third = step(norm_next, last)
    return (
        -c * (first + second * along[0] + third * last[0]),
        -c * (second * along[1] + third * last[1]),
        -c * (third * last[2]),
    )


def kernel(
    sizes,
    cells,
    state,
    explicit,
    implicit,
    coef,
    u_out,
    rms_out,
    state_in,
    explicit_in,
    implicit_in,
    b_send,
    d_send,
    field,
    weight,
    v0,
    v1,
    v2,
    u_send,
    u_home,
    relay,
    rows,
    own_rows,
    in_sem,
    out_sem,
    send_sem,
    relay_send,
    recv_sem,
    relay_recv,
    halo_send,
    halo_recv,
    row_send,
    row_recv,
):
    count_y, count_z = sizes
    groups = count_y * count_z
    y, z, x, core = (lax.axis_index(a) for a in AXES)
    place = 2 * x + core
    group = y * count_z + z
    right, left, across = lax.rem(x + 1, 4), lax.rem(x + 3, 4), lax.rem(x + 2, 4)

    def at(of_group, of_x, of_core):
        return (of_group // count_z, lax.rem(of_group, count_z), of_x, of_core)

    def in_ring(of_x, of_core):
        return (y, z, of_x, of_core)

    order = (
        (across, 0),
        (across, 1),
        (right, 0),
        (left, 0),
        (right, 1),
        (left, 1),
        (x, 1 - core),
        (x, core),
    )

    loads = []
    for k, (ox, oc) in enumerate(order):
        s = 2 * ox + oc
        loads.append(
            (
                pltpu.make_async_copy(state.at[s, 0], state_in.at[k], in_sem.at[k, 0]),
                pltpu.make_async_copy(explicit.at[:, s, 0], explicit_in.at[k], in_sem.at[k, 1]),
                pltpu.make_async_copy(implicit.at[:, s, 0], implicit_in.at[k], in_sem.at[k, 2]),
            )
        )
        for copy in loads[-1]:
            copy.start()

    barrier = pltpu.get_barrier_semaphore()

    def greet_far(k, _):
        other = lax.rem(group + k, groups)
        pl.semaphore_signal(
            barrier, inc=1, device_id=at(other, x, core), device_id_type=MESH
        )
        return _

    def greet_near(k, _):
        other = lax.rem(place + k, RING)
        pl.semaphore_signal(
            barrier,
            inc=1,
            device_id=in_ring(other // 2, lax.rem(other, 2)),
            device_id_type=MESH,
        )
        return _

    lax.fori_loop(1, RING, greet_near, 0)
    lax.fori_loop(1, groups, greet_far, 0)
    pl.semaphore_wait(barrier, groups - 1 + RING - 1)

    sent = []

    def spread(phase, k, source, target):
        if k < 2:
            copy = remote(
                source,
                relay.at[phase, k],
                send_sem.at[phase, k],
                relay_recv.at[phase, k],
                in_ring(right if k == 0 else left, core),
            )
        else:
            copy = remote(
                source,
                target,
                send_sem.at[phase, k],
                recv_sem.at[phase, place],
                in_ring(*order[k]),
            )
        copy.start()
        sent.append(copy)

    def forward(phase, target):
        for k in range(2):
            origin = 2 * (left if k == 0 else right) + core
            slot = relay.at[phase, k]
            pltpu.make_async_remote_copy(
                slot, slot, send_sem.at[phase, k], relay_recv.at[phase, k],
                device_id=in_ring(right, core), device_id_type=MESH,
            ).wait_recv()
            copy = remote(
                slot,
                target(origin),
                relay_send.at[phase, k],
                recv_sem.at[phase, origin],
                in_ring(right if k == 0 else left, k),
            )
            copy.start()
            sent.append(copy)

    def arrived(phase, target, origin):
        slot = target(origin)
        pltpu.make_async_remote_copy(
            slot, slot, send_sem.at[phase, 0], recv_sem.at[phase, origin],
            device_id=in_ring(right, core), device_id_type=MESH,
        ).wait_recv()

    def in_field(origin):
        return field.at[HALO + origin]

    def in_weight(origin):
        return weight.at[origin]

    def at_home(origin):
        return u_home.at[origin]

    def pass_on(origin):
        side = 2 * (origin // HALO) - 1
        slot = lax.rem(origin + HALO + RING, HALO + RING + HALO)
        copy = remote(
            field.at[HALO + origin],
            field.at[slot],
            halo_send.at[origin],
            halo_recv.at[slot],
            at(lax.rem(group + side + groups, groups), x, core),
        )
        copy.start()
        sent.append(copy)

    for k in range(RING):
        for copy in loads[k]:
            copy.wait()
        b = (
            state_in[k]
            + explicit_weights[0] * explicit_in[k, 0]
            + explicit_weights[1] * explicit_in[k, 1]
        )
        b = b + implicit_weights[0] * implicit_in[k, 0] + implicit_weights[1] * implicit_in[k, 1]
        if k < RING - 1:
            b_send[k] = b
            spread(0, k, b_send.at[k], in_field(place))
        else:
            field[HALO + place] = b
            pass_on(place)
    forward(0, in_field)
    for k in range(RING):
        d = 1.0 / (1.0 + 0.1 * jnp.abs(state_in[k]))
        if k < RING - 1:
            d_send[k] = d * d
            spread(1, k, d_send.at[k], in_weight(place))
        else:
            weight[place] = d * d
    for ox, oc in (order[6], order[2], order[3], order[4], order[5], order[0], order[1]):
        origin = 2 * ox + oc
        arrived(0, in_field, origin)
        pass_on(origin)
    forward(1, in_weight)
    for slot in (*range(HALO), *range(HALO + RING, HALO + RING + HALO)):
        place_of = field.at[slot]
        pltpu.make_async_remote_copy(
            place_of, place_of, halo_send.at[0], halo_recv.at[slot],
            device_id=in_ring(right, core), device_id_type=MESH,
        ).wait_recv()

    last = 2 * HALO + RING - 1
    low, high = HALO, HALO + RING

    def plane(ref, j, shift):
        return laplace(ref[j - 1], ref[j], ref[j + 1], shift)

    def first_pass(j, _):
        v0[j] = plane(field, j, 0.0)
        return _

    lax.fori_loop(1, last, first_pass, 0)

    def edge_pass(source, target):
        def body(j, _):
            target[j] = plane(source, j, SHIFT)
            return _

        return body

    def dot_pass(source, target):
        def body(j, sums):
            here = source[j]
            image = plane(source, j, SHIFT)
            if target is not None:
                target[j] = image
            return (sums[0] + folded(here * here), sums[1] + folded(here * image))

        return body

    zero = jnp.zeros((8, field.shape[-1]), jnp.float32)
    sums = []
    lax.fori_loop(2, low, edge_pass(v0, v1), 0)
    sums += lax.fori_loop(low, high, dot_pass(v0, v1), (zero, zero))
    lax.fori_loop(high, last - 1, edge_pass(v0, v1), 0)
    lax.fori_loop(3, low, edge_pass(v1, v2), 0)
    sums += lax.fori_loop(low, high, dot_pass(v1, v2), (zero, zero))
    lax.fori_loop(high, last - 2, edge_pass(v1, v2), 0)
    sums += lax.fori_loop(low, high, dot_pass(v2, None), (zero, zero))

    def publish(phase, values):
        row = row_of(values)
        own_rows[phase] = row
        rows[phase, group] = row

        def send(k, _):
            other = lax.rem(group + k, groups)
            remote(
                own_rows.at[phase],
                rows.at[phase, group],
                row_send.at[phase],
                row_recv.at[phase],
                at(other, x, core),
            ).start()
            return _

        lax.fori_loop(1, groups, send, 0)

    def total(phase, count):
        others = rows.at[phase, pl.ds(0, count - 1)]
        pltpu.make_async_remote_copy(
            others, others, row_send.at[phase], row_recv.at[phase],
            device_id=in_ring(right, core), device_id_type=MESH,
        ).wait_recv()
        row = rows[phase, 0]
        for k in range(1, count):
            row = row + rows[phase, k]
        return row

    def rows_sent(phase, count):
        others = rows.at[phase, pl.ds(0, count - 1)]
        pltpu.make_async_remote_copy(
            others, others, row_send.at[phase], row_recv.at[phase],
            device_id=in_ring(right, core), device_id_type=MESH,
        ).wait_send()

    publish(0, sums)

    for ox, oc in order[:7]:
        arrived(1, in_weight, 2 * ox + oc)

    def weighted(j, sums):
        d = weight[j - low]
        a, b, e = v0[j], v1[j], v2[j]
        da, db, de = d * a, d * b, d * e
        products = (da * a, da * b, da * e, db * b, db * e, de * e)
        return tuple(total + folded(product) for total, product in zip(sums, products))

    publish(1, lax.fori_loop(low, high, weighted, (zero,) * 6))

    c = coef[place]
    nu = entries(total(0, groups), MOMENTS)
    factor = basis_steps(nu, c)

    for k, (ox, oc) in enumerate(order):
        q = 2 * ox + oc
        j = low + q
        u = field[j] + (factor[0] * v0[j] + (factor[1] * v1[j] + factor[2] * v2[j]))
        if k < RING - 1:
            u_send[k] = u
            spread(2, k, u_send.at[k], at_home(place))
        else:
            u_home[place] = u

    out = []

    def write(s):
        copy = pltpu.make_async_copy(u_home.at[s], u_out.at[s, 0], out_sem.at[s])
        copy.start()
        out.append(copy)

    write(place)
    forward(2, at_home)

    g = entries(total(1, groups), 6)
    own = (
        factor[0] * factor[0] * g[0]
        + factor[1] * factor[1] * g[3]
        + factor[2] * factor[2] * g[5]
        + 2.0 * (factor[0] * factor[1] * g[1] + factor[0] * factor[2] * g[2] + factor[1] * factor[2] * g[4])
    )
    row = jnp.broadcast_to(own, (1, 128))
    own_rows[2] = row
    rows[2, place] = row

    def send_last(k, _):
        other = lax.rem(place + k, RING)
        remote(
            own_rows.at[2],
            rows.at[2, place],
            row_send.at[2],
            row_recv.at[2],
            in_ring(other // 2, lax.rem(other, 2)),
        ).start()
        return _

    lax.fori_loop(1, RING, send_last, 0)

    for ox, oc in (order[6], order[2], order[3], order[4], order[5], order[0], order[1]):
        s = 2 * ox + oc
        arrived(2, at_home, s)
        write(s)

    rms_out[...] = jnp.sqrt(total(2, RING)[0:1, 0:1] / cells)
    for copy in out:
        copy.wait()
    for copy in sent:
        copy.wait_send()
    rows_sent(0, groups)
    rows_sent(1, groups)
    rows_sent(2, RING)


def shards(state, explicit_rhs, implicit_rhs, implicit_coef):
    species, _, ny, nx = state.shape
    sizes = (lax.axis_size(AXES[0]), lax.axis_size(AXES[1]))
    groups = sizes[0] * sizes[1]
    cells = species * ny * nx * groups * RING
    depth = RING + 2 * HALO
    f32 = jnp.float32
    any_space = pl.BlockSpec(memory_space=pl.ANY)
    dma = pltpu.SemaphoreType.DMA
    u, rms = pl.pallas_call(
        functools.partial(kernel, sizes, cells),
        out_shape=(
            jax.ShapeDtypeStruct(state.shape, f32),
            jax.ShapeDtypeStruct((1, 1), f32),
        ),
        in_specs=[any_space] * 3 + [pl.BlockSpec(memory_space=pltpu.SMEM)],
        out_specs=(any_space, pl.BlockSpec(memory_space=pltpu.VMEM)),
        scratch_shapes=[
            pltpu.VMEM((RING, ny, nx), f32),
            pltpu.VMEM((RING, 2, ny, nx), f32),
            pltpu.VMEM((RING, 2, ny, nx), f32),
            pltpu.VMEM((RING, ny, nx), f32),
            pltpu.VMEM((RING, ny, nx), f32),
            pltpu.VMEM((depth, ny, nx), f32),
            pltpu.VMEM((RING, ny, nx), f32),
            pltpu.VMEM((depth, ny, nx), f32),
            pltpu.VMEM((depth, ny, nx), f32),
            pltpu.VMEM((depth, ny, nx), f32),
            pltpu.VMEM((RING, ny, nx), f32),
            pltpu.VMEM((RING, ny, nx), f32),
            pltpu.VMEM((3, 2, ny, nx), f32),
            pltpu.VMEM((3, max(groups, RING), 1, 128), f32),
            pltpu.VMEM((3, 1, 128), f32),
            dma((RING, 3)),
            dma((RING,)),
            dma((3, RING)),
            dma((3, 2)),
            dma((3, RING)),
            dma((3, 2)),
            dma((RING,)),
            dma((depth,)),
            dma((3,)),
            dma((3,)),
        ],
        compiler_params=pltpu.CompilerParams(collective_id=0, has_side_effects=True),
        name="section",
    )(state, explicit_rhs, implicit_rhs, implicit_coef)
    return u, rms[0, 0]


def solution(mesh):
    torus = Mesh(mesh.devices.reshape(-1, 8, 4, 2), AXES)
    placed = (
        P(None, AXES, None, None),
        P(None, None, AXES, None, None),
        P(None, None, AXES, None, None),
        P(),
    )
    return jax.shard_map(
        shards,
        mesh=torus,
        in_specs=placed,
        out_specs=(P(None, AXES, None, None), P()),
        check_vma=False,
    )
```

time: 168 us -> 52.7 us (0.31)
  blocking collectives: 113 us -> 0 us
  Pallas kernels: 0 us -> 48.4 us
  waiting for transfers between devices: 27.2 us -> 0 us
  starting transfers between devices: 15.4 us -> 0 us
  other arithmetic: 7.86 us -> 0 us
    all_to_all x8 -> x0, blocking collectives: 113 us -> none  [copy_for_each(): return lax.all_to_all(copies, axis, split_axis=0, concat_axis=0, tiled=True)]
    pallas_call x0 -> x1, Pallas kernels: none -> 48.4 us  [shards(): pl.pallas_call(functools.partial(kernel, sizes, cells), out_shape=(jax.Sh...]
    ppermute x8 -> x0, waiting for transfers between devices: 27.2 us -> none  [the longest x4 19 us: extended(): lax.ppermute(lax.slice_in_dim(block, block.shape[dim] - width, None, axis...]
    ppermute x8 -> x0, starting transfers between devices: 15.4 us -> none  [the longest x4 7.89 us: extended(): lax.ppermute(lax.slice_in_dim(block, 0, width, axis=dim), axis, backward)]
    reduce_sum x12 -> x0, other arithmetic: 4.83 us -> none  [the longest x1 1.71 us: shards(): jnp.sum(scaled * scaled)]
    add x1 -> x0, other arithmetic: 1.87 us -> none  [shards(): section_in + implicit_weights[0] * implicit_rhs[0]]
    unnamed x4 -> x1, local copies, waits for them, and re-layouts: 0.01 us -> 1.87 us
  transfers between devices with their start and end apart: 8 -> 0, of which waited for: 8 -> 0; matrix products, arithmetic and copies ran while one was open for 0% -> 0% of each run, Pallas kernels for 0% -> 0%
where the time goes in v1:
time: 52.7 us; the launch traced here: 52.6 us
  Pallas kernels  48.4 us (92%)
  between operations  2.34 us (4%)
  local copies, waits for them, and re-layouts  1.87 us (4%)
    pallas_call x1, Pallas kernels, shards(): pl.pallas_call(functools.partial(kernel, sizes, cells), out_shape=(jax.Sh...  48.4 us
    unnamed x1, local copies, waits for them, and re-layouts  1.87 us

profile of v1, /device:TPU:1, one launch (start us, length us, event | category | flops | bytes accessed | tf_op | source)
XLA Modules:
  0.0 52.6 jit_solution(49572005087201718)
XLA Ops:
  0.6 48.4 %section.1 = (f32[8,1,64,256]{3,2,1,0:T(8,128)}, f32[1,1]{1,0:T(1,128)}) custom-call(f32[8,1,64,256]{3,2,1,0:T(8,128)} %state.1, f32[2,8,1,64,256]{4,3,2,1,0:T(8,128)} %explicit.1, f32[2,8,1,64,256]{4,3,2,1,0:T(8,128)} %implicit.1, f32[8]{0:T(128)} %coef.1), custom_call_target="tpu_custom_call" | custom-call | tf_op jit(solution)/shard_map/section/pallas_call | solution.py:468
  49.0 1.9 %copy.8 = f32[8,1,64,256]{3,2,1,0:T(8,128)} copy(f32[8,1,64,256]{3,2,1,0:T(8,128)} %get-tuple-element.8) | data formatting | bytes 1048576

commit v2 on v1

v2 whole, which is shorter than its diff:
```python
import functools

import jax
import jax.numpy as jnp
from jax import lax
from jax.experimental import pallas as pl
from jax.experimental.pallas import tpu as pltpu
from jax.sharding import Mesh
from jax.sharding import PartitionSpec as P

AXES = ("gz_0", "gz_1", "gz_2", "gz_3")
MESH = pl.DeviceIdType.MESH

explicit_weights = (5535828885825.0 / 10492691773637.0, 788022342437.0 / 10882634858940.0)
implicit_weights = (2746238789719.0 / 10658868560708.0, -640167445237.0 / 6845629431997.0)

HALO = 4
RING = 8
MOMENTS = 6
SHIFT = 8.0


def remote(src, dst, send, recv, device):
    return pltpu.make_async_remote_copy(
        src_ref=src,
        dst_ref=dst,
        send_sem=send,
        recv_sem=recv,
        device_id=device,
        device_id_type=MESH,
    )


def laplace(below, here, above, shift=0.0):
    ny, nx = here.shape
    row = lax.broadcasted_iota(jnp.int32, here.shape, 0)
    lane = lax.broadcasted_iota(jnp.int32, here.shape, 1)
    beside = below + above
    beside = beside + jnp.where(row == ny - 1, 0.0, pltpu.roll(here, ny - 1, 0))
    beside = beside + jnp.where(row == 0, 0.0, pltpu.roll(here, 1, 0))
    beside = beside + jnp.where(lane == nx - 1, 0.0, pltpu.roll(here, nx - 1, 1))
    beside = beside + jnp.where(lane == 0, 0.0, pltpu.roll(here, 1, 1))
    return (6.0 - shift) * here - beside


def folded(value):
    total = value[0:8]
    for at in range(8, value.shape[0], 8):
        total = total + value[at : at + 8]
    return total


def row_of(sums):
    row = lax.broadcasted_iota(jnp.int32, (8, 128), 0)
    lane = lax.broadcasted_iota(jnp.int32, (8, 128), 1)
    stacked = jnp.zeros((8, 128), jnp.float32)
    for k, value in enumerate(sums):
        halves = sum(value[:, at : at + 128] for at in range(0, value.shape[1], 128))
        stacked = jnp.where(row == k, jnp.sum(halves, axis=0, keepdims=True), stacked)
    each = jnp.where(row == lane, jnp.sum(stacked, axis=1, keepdims=True), 0.0)
    return jnp.sum(each, axis=0, keepdims=True)


def entries(row, count):
    lane = lax.broadcasted_iota(jnp.int32, (1, 128), 1)
    return [
        jnp.sum(jnp.where(lane == k, row, 0.0), axis=1, keepdims=True) for k in range(count)
    ]


def basis_steps(nu, c):
    diagonal = 1.0 + SHIFT * c

    def gram(p, shift):
        total = None
        for i, a in enumerate(p):
            for j, b in enumerate(p):
                term = a * b * nu[i + j + shift]
                total = term if total is None else total + term
        return total

    def step(norm, along):
        energy = jnp.maximum(diagonal * gram(along, 0) + c * gram(along, 1), norm)
        return jnp.where(norm > 0.0, norm / energy, 0.0)

    norm = nu[0]
    first = norm / (diagonal * nu[0] + c * nu[1])
    residual = (1.0 - first * diagonal, -first * c)
    norm_next = jnp.maximum(gram(residual, 0), 0.0)
    ratio = norm_next / norm
    along = (residual[0] + ratio, residual[1])
    second = step(norm_next, along)
    norm = norm_next
    image = (diagonal * along[0], diagonal * along[1] + c * along[0], c * along[1])
    residual = (
        residual[0] - second * image[0],
        residual[1] - second * image[1],
        -second * image[2],
    )
    norm_next = jnp.maximum(gram(residual, 0), 0.0)
    ratio = jnp.where(norm > 0.0, norm_next / norm, 0.0)
    last = (residual[0] + ratio * along[0], residual[1] + ratio * along[1], residual[2])
    third = step(norm_next, last)
    return (
        -c * (first + second * along[0] + third * last[0]),
        -c * (second * along[1] + third * last[1]),
        -c * (third * last[2]),
    )


def kernel(
    sizes,
    cells,
    state,
    explicit,
    implicit,
    coef,
    u_home,
    rms_out,
    state_in,
    explicit_in,
    implicit_in,
    coef_in,
    b_send,
    d_send,
    field,
    weight,
    v0,
    v1,
    v2,
    u_send,
    relay,
    rows,
    own_rows,
    in_sem,
    send_sem,
    relay_send,
    recv_sem,
    relay_recv,
    halo_send,
    halo_recv,
    row_send,
    row_recv,
    wave_sem,
):
    count_y, count_z = sizes
    groups = count_y * count_z
    y, z, x, core = (lax.axis_index(a) for a in AXES)
    place = 2 * x + core
    group = y * count_z + z
    right, left, across = lax.rem(x + 1, 4), lax.rem(x + 3, 4), lax.rem(x + 2, 4)

    def in_ring(of_x, of_core):
        return (y, z, of_x, of_core)

    def at_group(step):
        of_group = lax.rem(group + step + groups, groups)
        return (of_group // count_z, lax.rem(of_group, count_z), x, core)

    def away(step_y, step_z):
        return (lax.rem(y + step_y, count_y), lax.rem(z + step_z + count_z, count_z), x, core)

    partners = [(x, 1 - core)] + [
        (chip, c) for chip in (right, left, across) for c in (core, 1 - core)
    ]

    barrier = pltpu.get_barrier_semaphore()
    near = [in_ring(*p) for p in partners] + [at_group(1), at_group(-1)]
    near += [away(k, 0) for k in range(1, count_y)] + [away(0, 1), away(0, -1)]
    for device in near:
        pl.semaphore_signal(barrier, inc=1, device_id=device, device_id_type=MESH)

    loads = [
        pltpu.make_async_copy(state.at[:, 0], state_in, in_sem.at[0]),
        pltpu.make_async_copy(explicit.at[:, :, 0], explicit_in, in_sem.at[1]),
        pltpu.make_async_copy(implicit.at[:, :, 0], implicit_in, in_sem.at[2]),
        pltpu.make_async_copy(coef, coef_in, in_sem.at[3]),
    ]
    for copy in loads:
        copy.start()
    for copy in loads:
        copy.wait()

    def prepare(s, _):
        b = (
            state_in[s]
            + explicit_weights[0] * explicit_in[0, s]
            + explicit_weights[1] * explicit_in[1, s]
        )
        b_send[s] = b + (
            implicit_weights[0] * implicit_in[0, s] + implicit_weights[1] * implicit_in[1, s]
        )
        d = 1.0 / (1.0 + 0.1 * jnp.abs(state_in[s]))
        d_send[s] = d * d
        return _

    lax.fori_loop(0, RING, prepare, 0, unroll=2)
    field[HALO + place] = b_send[place]
    weight[place] = d_send[place]

    pl.semaphore_wait(barrier, len(near))

    waves = [[(0, 1), (0, -1)], [(0, 2), (0, -2)], [(0, 4)]]

    def wave(k):
        for step in waves[k]:
            pl.semaphore_signal(
                wave_sem.at[k], inc=1, device_id=away(*step), device_id_type=MESH
            )

    def after_wave(k):
        pl.semaphore_wait(wave_sem.at[k], len(waves[k]))

    wave(0)
    sent = []

    def issue(*args):
        copy = remote(*args)
        copy.start()
        sent.append(copy)

    def direct(phase, block, target, chip, c):
        number = 2 * chip + c
        issue(
            block(number),
            target.at[place],
            send_sem.at[phase, number],
            recv_sem.at[phase, place],
            in_ring(chip, c),
        )

    def first_leg(phase, block):
        for k, chip in ((0, right), (1, left)):
            number = 2 * across + k
            issue(
                block(number),
                relay.at[phase, k],
                send_sem.at[phase, number],
                relay_recv.at[phase, k],
                in_ring(chip, core),
            )

    def second_leg(phase, target):
        for k, source, chip in ((0, left, right), (1, right, left)):
            slot = relay.at[phase, k]
            origin = 2 * source + core
            remote(
                slot, slot, relay_send.at[phase, k], relay_recv.at[phase, k], in_ring(right, core)
            ).wait_recv()
            issue(
                slot,
                target.at[origin],
                relay_send.at[phase, k],
                recv_sem.at[phase, origin],
                in_ring(chip, k),
            )

    def spread(phase, block, target, between=None):
        first_leg(phase, block)
        direct(phase, block, target, x, 1 - core)
        direct(phase, block, target, right, core)
        direct(phase, block, target, left, core)
        if between is not None:
            between()

    def spread_rest(phase, block, target):
        direct(phase, block, target, right, 1 - core)
        direct(phase, block, target, left, 1 - core)

    def arrived(phase, target, chip, c):
        origin = 2 * chip + c
        slot = target.at[origin]
        remote(
            slot, slot, send_sem.at[phase, 0], recv_sem.at[phase, origin], in_ring(right, core)
        ).wait_recv()
        return origin

    own_planes = field.at[pl.ds(HALO, RING)]

    def pass_on(origin):
        side = 2 * (origin // HALO) - 1
        slot = lax.rem(origin + HALO + RING, HALO + RING + HALO)
        issue(
            own_planes.at[origin],
            field.at[slot],
            halo_send.at[origin],
            halo_recv.at[slot],
            at_group(side),
        )

    arrivals = (partners[0], partners[1], partners[3], partners[5], partners[6], partners[2], partners[4])

    spread(0, lambda n: b_send.at[n], own_planes, lambda: pass_on(place))
    second_leg(0, own_planes)
    spread_rest(0, lambda n: b_send.at[n], own_planes)
    spread(1, lambda n: d_send.at[n], weight)
    spread_rest(1, lambda n: d_send.at[n], weight)
    after_wave(0)
    wave(1)
    for chip, c in arrivals:
        pass_on(arrived(0, own_planes, chip, c))
    after_wave(1)
    wave(2)
    second_leg(1, weight)

    last = 2 * HALO + RING
    low, high = HALO, HALO + RING

    def planes(source, target, shift, start, stop):
        def body(j, _):
            target[j] = laplace(source[j - 1], source[j], source[j + 1], shift)
            return _

        lax.fori_loop(start, stop, body, 0, unroll=True)

    planes(field, v0, 0.0, low + 1, high - 1)
    planes(v0, v1, SHIFT, low + 2, high - 2)
    planes(v1, v2, SHIFT, low + 3, high - 3)
    for slot in (*range(low), *range(high, last)):
        place_of = field.at[slot]
        remote(
            place_of, place_of, halo_send.at[0], halo_recv.at[slot], in_ring(right, core)
        ).wait_recv()
    for depth, (source, target, shift) in enumerate(
        ((field, v0, 0.0), (v0, v1, SHIFT), (v1, v2, SHIFT)), 1
    ):
        planes(source, target, shift, depth, low + depth)
        planes(source, target, shift, high - depth, last - depth)

    zero = jnp.zeros((8, field.shape[-1]), jnp.float32)

    def moments(j, sums):
        a, b, e = v0[j], v1[j], v2[j]
        image = laplace(v2[j - 1], e, v2[j + 1], SHIFT)
        products = (a * a, a * b, b * b, b * e, e * e, e * image)
        return tuple(total + folded(product) for total, product in zip(sums, products))

    sums = lax.fori_loop(low, high, moments, (zero,) * MOMENTS, unroll=2)

    far = sorted(
        ((dy, dz) for dy in range(count_y) for dz in range(count_z) if (dy, dz) != (0, 0)),
        key=lambda d: -min(d[0], count_y - d[0]) - min(d[1], count_z - d[1]),
    )

    def publish(phase, values):
        row = row_of(values)
        own_rows[phase] = row
        rows[phase, group] = row
        for step in far:
            remote(
                own_rows.at[phase],
                rows.at[phase, group],
                row_send.at[phase],
                row_recv.at[phase],
                away(*step),
            ).start()

    def others(phase, count):
        some = rows.at[phase, pl.ds(0, count - 1)]
        return remote(
            some, some, row_send.at[phase], row_recv.at[phase], in_ring(right, core)
        )

    def total(phase, count):
        others(phase, count).wait_recv()
        parts = [rows[phase, k] for k in range(count)]
        while len(parts) > 1:
            parts = [a + b for a, b in zip(parts[::2], parts[1::2])]
        return parts[0]

    after_wave(2)
    publish(0, sums)

    for chip, c in arrivals:
        arrived(1, weight, chip, c)

    def weighted(j, sums):
        d = weight[j - low]
        a, b, e = v0[j], v1[j], v2[j]
        da, db, de = d * a, d * b, d * e
        products = (da * a, da * b, da * e, db * b, db * e, de * e)
        return tuple(total + folded(product) for total, product in zip(sums, products))

    publish(1, lax.fori_loop(low, high, weighted, (zero,) * MOMENTS, unroll=2))

    c = coef_in[place]
    nu = entries(total(0, groups), MOMENTS)
    factor = basis_steps(nu, c)

    def update(k, _):
        j = low + k
        u = field[j] + (factor[0] * v0[j] + (factor[1] * v1[j] + factor[2] * v2[j]))
        u_send[k] = u
        return _

    lax.fori_loop(0, RING, update, 0, unroll=2)
    u_home[place] = u_send[place]
    spread(2, lambda n: u_send.at[n], u_home)
    spread_rest(2, lambda n: u_send.at[n], u_home)
    second_leg(2, u_home)

    g = entries(total(1, groups), MOMENTS)
    own = (
        factor[0] * factor[0] * g[0]
        + factor[1] * factor[1] * g[3]
        + factor[2] * factor[2] * g[5]
        + 2.0 * (factor[0] * factor[1] * g[1] + factor[0] * factor[2] * g[2] + factor[1] * factor[2] * g[4])
    )
    row = jnp.broadcast_to(own, (1, 128))
    own_rows[2] = row
    rows[2, place] = row
    for p in partners:
        remote(
            own_rows.at[2], rows.at[2, place], row_send.at[2], row_recv.at[2], in_ring(*p)
        ).start()
    rms_out[...] = jnp.sqrt(total(2, RING)[0:1, 0:1] / cells)

    for chip, c in arrivals:
        arrived(2, u_home, chip, c)
    for copy in sent:
        copy.wait_send()
    others(0, groups).wait_send()
    others(1, groups).wait_send()
    others(2, RING).wait_send()


def shards(state, explicit_rhs, implicit_rhs, implicit_coef):
    species, _, ny, nx = state.shape
    sizes = (lax.axis_size(AXES[0]), lax.axis_size(AXES[1]))
    groups = sizes[0] * sizes[1]
    cells = species * ny * nx * groups * RING
    depth = RING + 2 * HALO
    f32 = jnp.float32
    hbm, vmem = (pl.BlockSpec(memory_space=m) for m in (pltpu.HBM, pltpu.VMEM))
    dma = pltpu.SemaphoreType.DMA
    u, rms = pl.pallas_call(
        functools.partial(kernel, sizes, cells),
        out_shape=(
            jax.ShapeDtypeStruct((species, ny, nx), f32),
            jax.ShapeDtypeStruct((1, 1), f32),
        ),
        in_specs=[hbm] * 4,
        out_specs=(vmem, vmem),
        scratch_shapes=[
            pltpu.VMEM((RING, ny, nx), f32),
            pltpu.VMEM((2, RING, ny, nx), f32),
            pltpu.VMEM((2, RING, ny, nx), f32),
            pltpu.SMEM((species,), f32),
            pltpu.VMEM((RING, ny, nx), f32),
            pltpu.VMEM((RING, ny, nx), f32),
            pltpu.VMEM((depth, ny, nx), f32),
            pltpu.VMEM((RING, ny, nx), f32),
            pltpu.VMEM((depth, ny, nx), f32),
            pltpu.VMEM((depth, ny, nx), f32),
            pltpu.VMEM((depth, ny, nx), f32),
            pltpu.VMEM((RING, ny, nx), f32),
            pltpu.VMEM((3, 2, ny, nx), f32),
            pltpu.VMEM((3, max(groups, RING), 1, 128), f32),
            pltpu.VMEM((3, 1, 128), f32),
            dma((4,)),
            dma((3, RING)),
            dma((3, 2)),
            dma((3, RING)),
            dma((3, 2)),
            dma((RING,)),
            dma((depth,)),
            dma((3,)),
            dma((3,)),
            pltpu.SemaphoreType.REGULAR((3,)),
        ],
        compiler_params=pltpu.CompilerParams(
            collective_id=0, has_side_effects=True, vmem_limit_bytes=24 * 2**20
        ),
        name="section",
    )(
        *(
            pltpu.with_memory_space_constraint(a, pltpu.HBM)
            for a in (state, explicit_rhs, implicit_rhs, implicit_coef)
        )
    )
    return u.reshape(state.shape), rms[0, 0]


def solution(mesh):
    torus = Mesh(mesh.devices.reshape(-1, 8, 4, 2), AXES)
    placed = (
        P(None, AXES, None, None),
        P(None, None, AXES, None, None),
        P(None, None, AXES, None, None),
        P(),
    )
    return jax.shard_map(
        shards,
        mesh=torus,
        in_specs=placed,
        out_specs=(P(None, AXES, None, None), P()),
        check_vma=False,
    )
```

time: 52.7 us -> 43.8 us (0.83)
  Pallas kernels: 48.4 us -> 40.5 us
  local copies, waits for them, and re-layouts: 1.87 us -> 0.8 us
    pallas_call x1, Pallas kernels: 48.4 us -> 40.5 us  [shards(): pl.pallas_call(functools.partial(kernel, sizes, cells), out_shape=(jax.Sh...]
    unnamed x1, local copies, waits for them, and re-layouts: 1.87 us -> 0.8 us
where the time goes in v2:
time: 43.8 us; the launch traced here: 43.7 us
  Pallas kernels  40.5 us (92%)
  between operations  2.33 us (5%)
  local copies, waits for them, and re-layouts  0.8 us (2%)
    pallas_call x1, Pallas kernels, shards(): pl.pallas_call(functools.partial(kernel, sizes, cells), out_shape=(jax.Sh...  40.5 us

profile of v2, /device:TPU:1, one launch (start us, length us, event | category | flops | bytes accessed | tf_op | source)
XLA Modules:
  0.0 43.7 jit_solution(12390454352190545544)
XLA Ops:
  0.6 40.5 %section.1 = (f32[8,64,256]{2,1,0:T(8,128)S(1)}, f32[1,1]{1,0:T(1,128)}) custom-call(f32[8,1,64,256]{3,2,1,0:T(8,128)} %state.1, f32[2,8,1,64,256]{4,3,2,1,0:T(8,128)} %explicit.1, f32[2,8,1,64,256]{4,3,2,1,0:T(8,128)} %implicit.1, f32[8]{0:T(128)} %coef.1), custom_call_target="tpu_custom_call" | custom-call | tf_op jit(solution)/shard_map/section/pallas_call | solution.py:436
  41.2 0.8 %copy.9 = f32[8,1,64,256]{3,2,1,0:T(8,128)} copy(f32[8,1,64,256]{3,2,1,0:T(8,128)S(1)} %bitcast.4) | data formatting | bytes 1048576

commit v3 on v2

--- a/solution.py
+++ b/solution.py
@@ -18,6 +18,7 @@
 RING = 8
 MOMENTS = 6
 SHIFT = 8.0
+EARLY = 24
 
 
 def remote(src, dst, send, recv, device):
@@ -128,30 +129,30 @@
     v0,
     v1,
     v2,
+    v_home,
     u_send,
-    relay,
     rows,
     own_rows,
+    factors,
     in_sem,
-    send_sem,
-    relay_send,
+    b_recv,
+    halo_recv,
+    sent_sem,
     recv_sem,
-    relay_recv,
-    halo_send,
-    halo_recv,
-    row_send,
+    row_sent,
     row_recv,
     wave_sem,
 ):
     count_y, count_z = sizes
     groups = count_y * count_z
+    ny = field.shape[1]
     y, z, x, core = (lax.axis_index(a) for a in AXES)
     place = 2 * x + core
     group = y * count_z + z
     right, left, across = lax.rem(x + 1, 4), lax.rem(x + 3, 4), lax.rem(x + 2, 4)
 
-    def in_ring(of_x, of_core):
-        return (y, z, of_x, of_core)
+    def in_ring(chip, c):
+        return (y, z, chip, c)
 
     def at_group(step):
         of_group = lax.rem(group + step + groups, groups)
@@ -160,9 +161,9 @@
     def away(step_y, step_z):
         return (lax.rem(y + step_y, count_y), lax.rem(z + step_z + count_z, count_z), x, core)
 
-    partners = [(x, 1 - core)] + [
-        (chip, c) for chip in (right, left, across) for c in (core, 1 - core)
-    ]
+    partner = (x, 1 - core)
+    outside = [(chip, c) for c in (core, 1 - core) for chip in (across, right, left)]
+    partners = [partner] + outside
 
     barrier = pltpu.get_barrier_semaphore()
     near = [in_ring(*p) for p in partners] + [at_group(1), at_group(-1)]
@@ -170,35 +171,77 @@
     for device in near:
         pl.semaphore_signal(barrier, inc=1, device_id=device, device_id_type=MESH)
 
-    loads = [
-        pltpu.make_async_copy(state.at[:, 0], state_in, in_sem.at[0]),
-        pltpu.make_async_copy(explicit.at[:, :, 0], explicit_in, in_sem.at[1]),
-        pltpu.make_async_copy(implicit.at[:, :, 0], implicit_in, in_sem.at[2]),
-        pltpu.make_async_copy(coef, coef_in, in_sem.at[3]),
-    ]
-    for copy in loads:
-        copy.start()
-    for copy in loads:
-        copy.wait()
-
-    def prepare(s, _):
-        b = (
-            state_in[s]
-            + explicit_weights[0] * explicit_in[0, s]
-            + explicit_weights[1] * explicit_in[1, s]
-        )
-        b_send[s] = b + (
-            implicit_weights[0] * implicit_in[0, s] + implicit_weights[1] * implicit_in[1, s]
-        )
-        d = 1.0 / (1.0 + 0.1 * jnp.abs(state_in[s]))
-        d_send[s] = d * d
-        return _
-
-    lax.fori_loop(0, RING, prepare, 0, unroll=2)
+    for k, chip in enumerate((across, right, left, x)):
+        pair = pl.ds(2 * chip, 2)
+        for source, target in (
+            (state.at[pair, 0], state_in.at[pair]),
+            (explicit.at[:, pair, 0], explicit_in.at[:, pair]),
+            (implicit.at[:, pair, 0], implicit_in.at[:, pair]),
+        ):
+            pltpu.make_async_copy(source, target, in_sem.at[k]).start()
+    coef_load = pltpu.make_async_copy(coef, coef_in, in_sem.at[4])
+    coef_load.start()
+
+    def section_in(k, chip):
+        ten = field.at[pl.ds(0, 10)]
+        pltpu.make_async_copy(ten, ten, in_sem.at[k]).wait()
+        for s in (2 * chip, 2 * chip + 1):
+            b = (
+                state_in[s]
+                + explicit_weights[0] * explicit_in[0, s]
+                + explicit_weights[1] * explicit_in[1, s]
+            )
+            b_send[s] = b + (
+                implicit_weights[0] * implicit_in[0, s]
+                + implicit_weights[1] * implicit_in[1, s]
+            )
+
+    BLOCK, HALO_BLOCK, WEIGHT, EARLY_ROWS, FACTORS, LATE_ROWS = range(6)
+
+    def issue(source, target, kind, recv, device):
+        remote(source, target, sent_sem.at[kind], recv, device).start()
+
+    def some_copies(of, kind, recv):
+        return remote(of, of, sent_sem.at[kind], recv, in_ring(right, core))
+
+    def send_b(chip, c):
+        issue(
+            b_send.at[2 * chip + c],
+            field.at[HALO + place],
+            BLOCK,
+            b_recv.at[place],
+            in_ring(chip, c),
+        )
+
+    def pass_on(origin):
+        half = origin // HALO
+        issue(
+            field.at[HALO + origin],
+            field.at[lax.rem(origin + HALO + RING, HALO + RING + HALO)],
+            HALO_BLOCK,
+            halo_recv.at[1 - half],
+            at_group(2 * half - 1),
+        )
+
+    def b_arrived(chip, c):
+        origin = 2 * chip + c
+        some_copies(field.at[HALO + origin], BLOCK, b_recv.at[origin]).wait_recv()
+        return origin
+
+    section_in(0, across)
+    pl.semaphore_wait(barrier, len(near))
+    send_b(across, core)
+    send_b(across, 1 - core)
+    section_in(1, right)
+    send_b(right, core)
+    section_in(2, left)
+    send_b(left, core)
+    section_in(3, x)
     field[HALO + place] = b_send[place]
-    weight[place] = d_send[place]
-
-    pl.semaphore_wait(barrier, len(near))
+    send_b(*partner)
+    send_b(right, 1 - core)
+    send_b(left, 1 - core)
+    pass_on(place)
 
     waves = [[(0, 1), (0, -1)], [(0, 2), (0, -2)], [(0, 4)]]
 
@@ -212,96 +255,40 @@
         pl.semaphore_wait(wave_sem.at[k], len(waves[k]))
 
     wave(0)
-    sent = []
-
-    def issue(*args):
-        copy = remote(*args)
-        copy.start()
-        sent.append(copy)
-
-    def direct(phase, block, target, chip, c):
+
+    def weigh(s, _):
+        d = 1.0 / (1.0 + 0.1 * jnp.abs(state_in[s]))
+        d_send[s] = d * d
+        return _
+
+    lax.fori_loop(0, RING, weigh, 0, unroll=2)
+    weight[place] = d_send[place]
+    pass_on(b_arrived(*partner))
+    for chip, c in partners:
         number = 2 * chip + c
         issue(
-            block(number),
-            target.at[place],
-            send_sem.at[phase, number],
-            recv_sem.at[phase, place],
+            d_send.at[number],
+            weight.at[place],
+            WEIGHT,
+            recv_sem.at[WEIGHT],
             in_ring(chip, c),
         )
-
-    def first_leg(phase, block):
-        for k, chip in ((0, right), (1, left)):
-            number = 2 * across + k
-            issue(
-                block(number),
-                relay.at[phase, k],
-                send_sem.at[phase, number],
-                relay_recv.at[phase, k],
-                in_ring(chip, core),
-            )
-
-    def second_leg(phase, target):
-        for k, source, chip in ((0, left, right), (1, right, left)):
-            slot = relay.at[phase, k]
-            origin = 2 * source + core
-            remote(
-                slot, slot, relay_send.at[phase, k], relay_recv.at[phase, k], in_ring(right, core)
-            ).wait_recv()
-            issue(
-                slot,
-                target.at[origin],
-                relay_send.at[phase, k],
-                recv_sem.at[phase, origin],
-                in_ring(chip, k),
-            )
-
-    def spread(phase, block, target, between=None):
-        first_leg(phase, block)
-        direct(phase, block, target, x, 1 - core)
-        direct(phase, block, target, right, core)
-        direct(phase, block, target, left, core)
-        if between is not None:
-            between()
-
-    def spread_rest(phase, block, target):
-        direct(phase, block, target, right, 1 - core)
-        direct(phase, block, target, left, 1 - core)
-
-    def arrived(phase, target, chip, c):
-        origin = 2 * chip + c
-        slot = target.at[origin]
-        remote(
-            slot, slot, send_sem.at[phase, 0], recv_sem.at[phase, origin], in_ring(right, core)
-        ).wait_recv()
-        return origin
-
-    own_planes = field.at[pl.ds(HALO, RING)]
-
-    def pass_on(origin):
-        side = 2 * (origin // HALO) - 1
-        slot = lax.rem(origin + HALO + RING, HALO + RING + HALO)
-        issue(
-            own_planes.at[origin],
-            field.at[slot],
-            halo_send.at[origin],
-            halo_recv.at[slot],
-            at_group(side),
-        )
-
-    arrivals = (partners[0], partners[1], partners[3], partners[5], partners[6], partners[2], partners[4])
-
-    spread(0, lambda n: b_send.at[n], own_planes, lambda: pass_on(place))
-    second_leg(0, own_planes)
-    spread_rest(0, lambda n: b_send.at[n], own_planes)
-    spread(1, lambda n: d_send.at[n], weight)
-    spread_rest(1, lambda n: d_send.at[n], weight)
-    after_wave(0)
-    wave(1)
-    for chip, c in arrivals:
-        pass_on(arrived(0, own_planes, chip, c))
+    for number, p in enumerate(
+        (
+            (across, core),
+            (across, 1 - core),
+            (right, core),
+            (left, core),
+            (right, 1 - core),
+            (left, 1 - core),
+        )
+    ):
+        pass_on(b_arrived(*p))
+        if number == 1:
+            after_wave(0)
+            wave(1)
     after_wave(1)
     wave(2)
-    second_leg(1, weight)
 
     last = 2 * HALO + RING
     low, high = HALO, HALO + RING
@@ -316,17 +303,6 @@
     planes(field, v0, 0.0, low + 1, high - 1)
     planes(v0, v1, SHIFT, low + 2, high - 2)
     planes(v1, v2, SHIFT, low + 3, high - 3)
-    for slot in (*range(low), *range(high, last)):
-        place_of = field.at[slot]
-        remote(
-            place_of, place_of, halo_send.at[0], halo_recv.at[slot], in_ring(right, core)
-        ).wait_recv()
-    for depth, (source, target, shift) in enumerate(
-        ((field, v0, 0.0), (v0, v1, SHIFT), (v1, v2, SHIFT)), 1
-    ):
-        planes(source, target, shift, depth, low + depth)
-        planes(source, target, shift, high - depth, last - depth)
-
     zero = jnp.zeros((8, field.shape[-1]), jnp.float32)
 
     def moments(j, sums):
@@ -335,7 +311,32 @@
         products = (a * a, a * b, b * b, b * e, e * e, e * image)
         return tuple(total + folded(product) for total, product in zip(sums, products))
 
-    sums = lax.fori_loop(low, high, moments, (zero,) * MOMENTS, unroll=2)
+    sums = (zero,) * MOMENTS
+    middle = low + RING // 2
+    for side, start, stop in (
+        (0, lambda d: d, lambda d: low + d),
+        (1, lambda d: high - d, lambda d: last - d),
+    ):
+        four = field.at[pl.ds(side * high, HALO)]
+        some_copies(four, HALO_BLOCK, halo_recv.at[side]).wait_recv()
+        planes(field, v0, 0.0, start(1), stop(1))
+        planes(v0, v1, SHIFT, start(2), stop(2))
+        planes(v1, v2, SHIFT, start(3), stop(3))
+        if side == 0:
+            sums = lax.fori_loop(low, middle, moments, sums, unroll=2)
+
+    for chip, c in outside + [partner]:
+        number = 2 * chip + c
+        for i, v in enumerate((v0, v1, v2)):
+            issue(
+                v.at[low + number, pl.ds(0, EARLY)],
+                v_home.at[place, i],
+                EARLY_ROWS,
+                recv_sem.at[EARLY_ROWS],
+                in_ring(chip, c),
+            )
+
+    sums = lax.fori_loop(middle, high, moments, sums, unroll=2)
 
     far = sorted(
         ((dy, dz) for dy in range(count_y) for dz in range(count_z) if (dy, dz) != (0, 0)),
@@ -350,7 +351,7 @@
             remote(
                 own_rows.at[phase],
                 rows.at[phase, group],
-                row_send.at[phase],
+                row_sent.at[phase],
                 row_recv.at[phase],
                 away(*step),
             ).start()
@@ -358,7 +359,7 @@
     def others(phase, count):
         some = rows.at[phase, pl.ds(0, count - 1)]
         return remote(
-            some, some, row_send.at[phase], row_recv.at[phase], in_ring(right, core)
+            some, some, row_sent.at[phase], row_recv.at[phase], in_ring(right, core)
         )
 
     def total(phase, count):
@@ -371,8 +372,20 @@
     after_wave(2)
     publish(0, sums)
 
-    for chip, c in arrivals:
-        arrived(1, weight, chip, c)
+    seven = pl.ds(0, RING - 1)
+    everything = {
+        BLOCK: b_send.at[seven],
+        HALO_BLOCK: field.at[pl.ds(0, RING)],
+        WEIGHT: weight.at[seven],
+        EARLY_ROWS: v_home.at[seven],
+        FACTORS: factors.at[seven],
+        LATE_ROWS: u_send.at[seven],
+    }
+
+    def all_copies(kind):
+        return some_copies(everything[kind], kind, recv_sem.at[kind])
+
+    all_copies(WEIGHT).wait_recv()
 
     def weighted(j, sums):
         d = weight[j - low]
@@ -382,46 +395,95 @@
         return tuple(total + folded(product) for total, product in zip(sums, products))
 
     publish(1, lax.fori_loop(low, high, weighted, (zero,) * MOMENTS, unroll=2))
-
-    c = coef_in[place]
+    coef_load.wait()
+
+    c_here = coef_in[place]
     nu = entries(total(0, groups), MOMENTS)
-    factor = basis_steps(nu, c)
+    factor = basis_steps(nu, c_here)
+    for i in range(3):
+        factors[place, i] = jnp.broadcast_to(factor[i], factors.shape[2:])
+
+    late = pl.ds(EARLY, ny - EARLY)
+
+    def combined(k, of_rows):
+        j = low + k
+        return field[j, of_rows] + (
+            factor[0] * v0[j, of_rows]
+            + (factor[1] * v1[j, of_rows] + factor[2] * v2[j, of_rows])
+        )
 
     def update(k, _):
-        j = low + k
-        u = field[j] + (factor[0] * v0[j] + (factor[1] * v1[j] + factor[2] * v2[j]))
-        u_send[k] = u
+        u_send[k] = combined(k, late)
         return _
 
     lax.fori_loop(0, RING, update, 0, unroll=2)
-    u_home[place] = u_send[place]
-    spread(2, lambda n: u_send.at[n], u_home)
-    spread_rest(2, lambda n: u_send.at[n], u_home)
-    second_leg(2, u_home)
+    for chip, c in partners:
+        issue(
+            factors.at[place],
+            factors.at[place],
+            FACTORS,
+            recv_sem.at[FACTORS],
+            in_ring(chip, c),
+        )
+    for chip, c in outside + [partner]:
+        number = 2 * chip + c
+        issue(
+            u_send.at[number],
+            u_home.at[place, late],
+            LATE_ROWS,
+            recv_sem.at[LATE_ROWS],
+            in_ring(chip, c),
+        )
+    early = pl.ds(0, EARLY)
+    u_home[place, late] = u_send[place]
+    u_home[place, early] = combined(place, early)
 
     g = entries(total(1, groups), MOMENTS)
     own = (
         factor[0] * factor[0] * g[0]
         + factor[1] * factor[1] * g[3]
         + factor[2] * factor[2] * g[5]
-        + 2.0 * (factor[0] * factor[1] * g[1] + factor[0] * factor[2] * g[2] + factor[1] * factor[2] * g[4])
+        + 2.0
+        * (
+            factor[0] * factor[1] * g[1]
+            + factor[0] * factor[2] * g[2]
+            + factor[1] * factor[2] * g[4]
+        )
     )
     row = jnp.broadcast_to(own, (1, 128))
     own_rows[2] = row
     rows[2, place] = row
     for p in partners:
         remote(
-            own_rows.at[2], rows.at[2, place], row_send.at[2], row_recv.at[2], in_ring(*p)
+            own_rows.at[2], rows.at[2, place], row_sent.at[2], row_recv.at[2], in_ring(*p)
         ).start()
+
+    all_copies(EARLY_ROWS).wait_recv()
+    all_copies(FACTORS).wait_recv()
+    for chip, c in partners:
+        s = 2 * chip + c
+        u_home[s, early] = b_send[s, early] + (
+            factors[s, 0] * v_home[s, 0]
+            + (factors[s, 1] * v_home[s, 1] + factors[s, 2] * v_home[s, 2])
+        )
     rms_out[...] = jnp.sqrt(total(2, RING)[0:1, 0:1] / cells)
-
-    for chip, c in arrivals:
-        arrived(2, u_home, chip, c)
-    for copy in sent:
-        copy.wait_send()
+    all_copies(LATE_ROWS).wait_recv()
+    for kind in everything:
+        all_copies(kind).wait_send()
     others(0, groups).wait_send()
     others(1, groups).wait_send()
     others(2, RING).wait_send()
+
+
+def deliver(u, rms, u_out, rms_out, sems):
+    copies = (
+        pltpu.make_async_copy(u, u_out, sems.at[0]),
+        pltpu.make_async_copy(rms, rms_out, sems.at[1]),
+    )
+    for copy in copies:
+        copy.start()
+    for copy in copies:
+        copy.wait()
 
 
 def shards(state, explicit_rhs, implicit_rhs, implicit_coef):
@@ -453,17 +515,16 @@
             pltpu.VMEM((depth, ny, nx), f32),
             pltpu.VMEM((depth, ny, nx), f32),
             pltpu.VMEM((depth, ny, nx), f32),
-            pltpu.VMEM((RING, ny, nx), f32),
-            pltpu.VMEM((3, 2, ny, nx), f32),
+            pltpu.VMEM((RING, 3, EARLY, nx), f32),
+            pltpu.VMEM((RING, ny - EARLY, nx), f32),
             pltpu.VMEM((3, max(groups, RING), 1, 128), f32),
             pltpu.VMEM((3, 1, 128), f32),
-            dma((4,)),
-            dma((3, RING)),
-            dma((3, 2)),
-            dma((3, RING)),
-            dma((3, 2)),
+            pltpu.VMEM((RING, 3, 1, nx), f32),
+            dma((5,)),
             dma((RING,)),
-            dma((depth,)),
+            dma((2,)),
+            dma((6,)),
+            dma((6,)),
             dma((3,)),
             dma((3,)),
             pltpu.SemaphoreType.REGULAR((3,)),
@@ -478,6 +539,15 @@
             for a in (state, explicit_rhs, implicit_rhs, implicit_coef)
         )
     )
+    u, rms = pl.pallas_call(
+        deliver,
+        out_shape=(jax.ShapeDtypeStruct(u.shape, f32), jax.ShapeDtypeStruct((1, 1), f32)),
+        in_specs=[vmem, vmem],
+        out_specs=(hbm, hbm),
+        scratch_shapes=[dma((2,))],
+        compiler_params=pltpu.CompilerParams(vmem_limit_bytes=2**20),
+        name="deliver",
+    )(u, rms)
     return u.reshape(state.shape), rms[0, 0]
 
 

time: 43.8 us -> 40 us (0.913)
  between operations: 2.33 us -> 0.64 us
  Pallas kernels: 40.5 us -> 39.2 us
  local copies, waits for them, and re-layouts: 0.8 us -> 0 us
    pallas_call x1, Pallas kernels: 40.5 us -> 37.8 us  [shards(): pl.pallas_call(functools.partial(kernel, sizes, cells), out_shape=(jax.Sh...]
    pallas_call x0 -> x1, Pallas kernels: none -> 1.45 us  [shards(): pl.pallas_call(deliver, out_shape=(jax.ShapeDtypeStruct(u.shape, f32), ja...]
    unnamed x1 -> x0, local copies, waits for them, and re-layouts: 0.8 us -> none
where the time goes in v3:
time: 40 us; the launch traced here: 39.9 us
  Pallas kernels  39.2 us (98%)
  between operations  0.64 us (2%)
    pallas_call x1, Pallas kernels, shards(): pl.pallas_call(functools.partial(kernel, sizes, cells), out_shape=(jax.Sh...  37.8 us
    pallas_call x1, Pallas kernels, shards(): pl.pallas_call(deliver, out_shape=(jax.ShapeDtypeStruct(u.shape, f32), ja...  1.45 us

profile of v3, /device:TPU:1, one launch (start us, length us, event | category | flops | bytes accessed | tf_op | source)
XLA Modules:
  0.0 39.9 jit_solution(338742046001668220)
XLA Ops:
  0.6 37.8 %section.1 = (f32[8,64,256]{2,1,0:T(8,128)S(1)}, f32[1,1]{1,0:T(1,128)}) custom-call(f32[8,1,64,256]{3,2,1,0:T(8,128)} %state.1, f32[2,8,1,64,256]{4,3,2,1,0:T(8,128)} %explicit.1, f32[2,8,1,64,256]{4,3,2,1,0:T(8,128)} %implicit.1, f32[8]{0:T(128)} %coef.1), custom_call_target="tpu_custom_call" | custom-call | tf_op jit(solution)/shard_map/section/pallas_call | solution.py:498
  38.4 1.4 %deliver.1 = (f32[8,64,256]{2,1,0:T(8,128)}, f32[1,1]{1,0:T(1,128)}) custom-call(f32[8,64,256]{2,1,0:T(8,128)S(1)} %get-tuple-element.6.u, f32[1,1]{1,0:T(1,128)} %get-tuple-element.7.rms), custom_call_target="tpu_custom_call" | custom-call | tf_op jit(solution)/shard_map/deliver/pallas_call | solution.py:542

commit v4 on v3

--- a/solution.py
+++ b/solution.py
@@ -18,7 +18,7 @@
 RING = 8
 MOMENTS = 6
 SHIFT = 8.0
-EARLY = 24
+EARLY = 16
 
 
 def remote(src, dst, send, recv, device):
@@ -151,8 +151,14 @@
     group = y * count_z + z
     right, left, across = lax.rem(x + 1, 4), lax.rem(x + 3, 4), lax.rem(x + 2, 4)
 
+    flip = x // 2
+
     def in_ring(chip, c):
         return (y, z, chip, c)
+
+    def layer(number, chip):
+        turned = chip // 2
+        return turned * (RING - 1) + (1 - 2 * turned) * number
 
     def at_group(step):
         of_group = lax.rem(group + step + groups, groups)
@@ -166,8 +172,8 @@
     partners = [partner] + outside
 
     barrier = pltpu.get_barrier_semaphore()
-    near = [in_ring(*p) for p in partners] + [at_group(1), at_group(-1)]
-    near += [away(k, 0) for k in range(1, count_y)] + [away(0, 1), away(0, -1)]
+    beside = [away(0, 1), away(0, -1), away(1, 0), away(count_y - 1, 0)]
+    near = [in_ring(*p) for p in partners] + beside
     for device in near:
         pl.semaphore_signal(barrier, inc=1, device_id=device, device_id_type=MESH)
 
@@ -207,48 +213,51 @@
     def send_b(chip, c):
         issue(
             b_send.at[2 * chip + c],
-            field.at[HALO + place],
+            field.at[HALO + layer(place, chip)],
             BLOCK,
             b_recv.at[place],
             in_ring(chip, c),
         )
 
-    def pass_on(origin):
+    def pass_on(number):
+        origin = layer(number, x)
         half = origin // HALO
-        issue(
-            field.at[HALO + origin],
-            field.at[lax.rem(origin + HALO + RING, HALO + RING + HALO)],
-            HALO_BLOCK,
-            halo_recv.at[1 - half],
-            at_group(2 * half - 1),
-        )
+
+        @pl.when(origin != HALO)
+        def _():
+            issue(
+                field.at[HALO + origin],
+                field.at[lax.rem(origin + HALO + RING, HALO + RING + HALO)],
+                HALO_BLOCK,
+                halo_recv.at[1 - half],
+                at_group((2 * half - 1) * (1 - 2 * flip)),
+            )
 
     def b_arrived(chip, c):
-        origin = 2 * chip + c
-        some_copies(field.at[HALO + origin], BLOCK, b_recv.at[origin]).wait_recv()
-        return origin
+        number = 2 * chip + c
+        some_copies(field.at[HALO + layer(number, x)], BLOCK, b_recv.at[number]).wait_recv()
+        return number
 
     section_in(0, across)
     pl.semaphore_wait(barrier, len(near))
     send_b(across, core)
-    send_b(across, 1 - core)
     section_in(1, right)
     send_b(right, core)
     section_in(2, left)
     send_b(left, core)
+    send_b(across, 1 - core)
     section_in(3, x)
-    field[HALO + place] = b_send[place]
+    field[HALO + layer(place, x)] = b_send[place]
     send_b(*partner)
     send_b(right, 1 - core)
     send_b(left, 1 - core)
-    pass_on(place)
-
-    waves = [[(0, 1), (0, -1)], [(0, 2), (0, -2)], [(0, 4)]]
+
+    waves = [beside, [away(0, k) for k in (1, -1, 2, -2)], [away(0, 2), away(0, -2)]]
 
     def wave(k):
-        for step in waves[k]:
+        for device in waves[k]:
             pl.semaphore_signal(
-                wave_sem.at[k], inc=1, device_id=away(*step), device_id_type=MESH
+                wave_sem.at[k], inc=1, device_id=device, device_id_type=MESH
             )
 
     def after_wave(k):
@@ -262,31 +271,29 @@
         return _
 
     lax.fori_loop(0, RING, weigh, 0, unroll=2)
-    weight[place] = d_send[place]
-    pass_on(b_arrived(*partner))
+    weight[layer(place, x)] = d_send[place]
     for chip, c in partners:
         number = 2 * chip + c
         issue(
             d_send.at[number],
-            weight.at[place],
+            weight.at[layer(place, chip)],
             WEIGHT,
             recv_sem.at[WEIGHT],
             in_ring(chip, c),
         )
-    for number, p in enumerate(
-        (
-            (across, core),
-            (across, 1 - core),
-            (right, core),
-            (left, core),
-            (right, 1 - core),
-            (left, 1 - core),
-        )
+    after_wave(0)
+    wave(1)
+    pass_on(place)
+    pass_on(b_arrived(*partner))
+    for p in (
+        (across, core),
+        (right, core),
+        (left, core),
+        (across, 1 - core),
+        (right, 1 - core),
+        (left, 1 - core),
     ):
         pass_on(b_arrived(*p))
-        if number == 1:
-            after_wave(0)
-            wave(1)
     after_wave(1)
     wave(2)
 
@@ -307,18 +314,18 @@
 
     def moments(j, sums):
         a, b, e = v0[j], v1[j], v2[j]
-        image = laplace(v2[j - 1], e, v2[j + 1], SHIFT)
+        image = laplace(v2[j + 1], e, v2[j + 1], SHIFT)
         products = (a * a, a * b, b * b, b * e, e * e, e * image)
         return tuple(total + folded(product) for total, product in zip(sums, products))
 
     sums = (zero,) * MOMENTS
     middle = low + RING // 2
     for side, start, stop in (
-        (0, lambda d: d, lambda d: low + d),
+        (0, lambda d: d + 1, lambda d: low + d),
         (1, lambda d: high - d, lambda d: last - d),
     ):
-        four = field.at[pl.ds(side * high, HALO)]
-        some_copies(four, HALO_BLOCK, halo_recv.at[side]).wait_recv()
+        blocks = field.at[pl.ds(1, 3) if side == 0 else pl.ds(high, HALO)]
+        some_copies(blocks, HALO_BLOCK, halo_recv.at[side]).wait_recv()
         planes(field, v0, 0.0, start(1), stop(1))
         planes(v0, v1, SHIFT, start(2), stop(2))
         planes(v1, v2, SHIFT, start(3), stop(3))
@@ -329,7 +336,7 @@
         number = 2 * chip + c
         for i, v in enumerate((v0, v1, v2)):
             issue(
-                v.at[low + number, pl.ds(0, EARLY)],
+                v.at[low + layer(number, x), pl.ds(0, EARLY)],
                 v_home.at[place, i],
                 EARLY_ROWS,
                 recv_sem.at[EARLY_ROWS],
@@ -375,7 +382,7 @@
     seven = pl.ds(0, RING - 1)
     everything = {
         BLOCK: b_send.at[seven],
-        HALO_BLOCK: field.at[pl.ds(0, RING)],
+        HALO_BLOCK: field.at[seven],
         WEIGHT: weight.at[seven],
         EARLY_ROWS: v_home.at[seven],
         FACTORS: factors.at[seven],
@@ -428,15 +435,16 @@
     for chip, c in outside + [partner]:
         number = 2 * chip + c
         issue(
-            u_send.at[number],
+            u_send.at[layer(number, x)],
             u_home.at[place, late],
             LATE_ROWS,
             recv_sem.at[LATE_ROWS],
             in_ring(chip, c),
         )
     early = pl.ds(0, EARLY)
-    u_home[place, late] = u_send[place]
-    u_home[place, early] = combined(place, early)
+    mine = layer(place, x)
+    u_home[place, late] = u_send[mine]
+    u_home[place, early] = combined(mine, early)
 
     g = entries(total(1, groups), MOMENTS)
     own = (
@@ -466,7 +474,7 @@
             factors[s, 0] * v_home[s, 0]
             + (factors[s, 1] * v_home[s, 1] + factors[s, 2] * v_home[s, 2])
         )
-    rms_out[...] = jnp.sqrt(total(2, RING)[0:1, 0:1] / cells)
+    rms_out[...] = jnp.broadcast_to(jnp.sqrt(total(2, RING) / cells), rms_out.shape)
     all_copies(LATE_ROWS).wait_recv()
     for kind in everything:
         all_copies(kind).wait_send()
@@ -475,13 +483,17 @@
     others(2, RING).wait_send()
 
 
-def deliver(u, rms, u_out, rms_out, sems):
-    copies = (
-        pltpu.make_async_copy(u, u_out, sems.at[0]),
-        pltpu.make_async_copy(rms, rms_out, sems.at[1]),
-    )
-    for copy in copies:
+def deliver(u, rms, u_out, rms_out, rms_row, sems):
+    per = u.shape[0] // 1
+    copies = [
+        pltpu.make_async_copy(u.at[pl.ds(k * per, per)], u_out.at[pl.ds(k * per, per)], sems.at[k])
+        for k in range(1)
+    ]
+    copies.append(pltpu.make_async_copy(rms_row, rms_out, sems.at[1]))
+    for copy in copies[:-1]:
         copy.start()
+    rms_row[...] = rms[0:1, 0:1]
+    copies[-1].start()
     for copy in copies:
         copy.wait()
 
@@ -499,7 +511,7 @@
         functools.partial(kernel, sizes, cells),
         out_shape=(
             jax.ShapeDtypeStruct((species, ny, nx), f32),
-            jax.ShapeDtypeStruct((1, 1), f32),
+            jax.ShapeDtypeStruct((8, 128), f32),
         ),
         in_specs=[hbm] * 4,
         out_specs=(vmem, vmem),
@@ -544,7 +556,7 @@
         out_shape=(jax.ShapeDtypeStruct(u.shape, f32), jax.ShapeDtypeStruct((1, 1), f32)),
         in_specs=[vmem, vmem],
         out_specs=(hbm, hbm),
-        scratch_shapes=[dma((2,))],
+        scratch_shapes=[pltpu.VMEM((1, 1), f32), dma((2,))],
         compiler_params=pltpu.CompilerParams(vmem_limit_bytes=2**20),
         name="deliver",
     )(u, rms)

time: 40 us -> 37.2 us (0.930)
  Pallas kernels: 39.2 us -> 36.5 us
    pallas_call x1, Pallas kernels: 37.8 us -> 35.7 us  [shards(): pl.pallas_call(functools.partial(kernel, sizes, cells), out_shape=(jax.Sh...]
    pallas_call x1, Pallas kernels: 1.45 us -> 0.81 us  [shards(): pl.pallas_call(deliver, out_shape=(jax.ShapeDtypeStruct(u.shape, f32), ja...]
where the time goes in v4:
time: 37.2 us; the launch traced here: 37.1 us
  Pallas kernels  36.5 us (98%)
  between operations  0.64 us (2%)
    pallas_call x1, Pallas kernels, shards(): pl.pallas_call(functools.partial(kernel, sizes, cells), out_shape=(jax.Sh...  35.7 us
    pallas_call x1, Pallas kernels, shards(): pl.pallas_call(deliver, out_shape=(jax.ShapeDtypeStruct(u.shape, f32), ja...  0.81 us

profile of v4, /device:TPU:1, one launch (start us, length us, event | category | flops | bytes accessed | tf_op | source)
XLA Modules:
  0.0 37.1 jit_solution(9903587992818896903)
XLA Ops:
  0.6 35.7 %section.1 = (f32[8,64,256]{2,1,0:T(8,128)S(1)}, f32[8,128]{1,0:T(8,128)S(1)}) custom-call(f32[8,1,64,256]{3,2,1,0:T(8,128)} %state.1, f32[2,8,1,64,256]{4,3,2,1,0:T(8,128)} %explicit.1, f32[2,8,1,64,256]{4,3,2,1,0:T(8,128)} %implicit.1, f32[8]{0:T(128)} %coef.1), custom_call_target="tpu_custom_call" | custom-call | tf_op jit(solution)/shard_map/section/pallas_call | solution.py:510
  36.3 0.8 %deliver.1 = (f32[8,64,256]{2,1,0:T(8,128)}, f32[1,1]{1,0:T(1,128)}) custom-call(f32[8,64,256]{2,1,0:T(8,128)S(1)} %get-tuple-element.6.u, f32[8,128]{1,0:T(8,128)S(1)} %get-tuple-element.7.rms), custom_call_target="tpu_custom_call" | custom-call | tf_op jit(solution)/shard_map/deliver/pallas_call | solution.py:554

commit v5 on v4

--- a/solution.py
+++ b/solution.py
@@ -272,6 +272,12 @@
 
     lax.fori_loop(0, RING, weigh, 0, unroll=2)
     weight[layer(place, x)] = d_send[place]
+    after_wave(0)
+    wave(1)
+    pass_on(place)
+    pass_on(b_arrived(*partner))
+    for p in ((across, core), (right, core), (left, core), (across, 1 - core)):
+        pass_on(b_arrived(*p))
     for chip, c in partners:
         number = 2 * chip + c
         issue(
@@ -281,18 +287,7 @@
             recv_sem.at[WEIGHT],
             in_ring(chip, c),
         )
-    after_wave(0)
-    wave(1)
-    pass_on(place)
-    pass_on(b_arrived(*partner))
-    for p in (
-        (across, core),
-        (right, core),
-        (left, core),
-        (across, 1 - core),
-        (right, 1 - core),
-        (left, 1 - core),
-    ):
+    for p in ((right, 1 - core), (left, 1 - core)):
         pass_on(b_arrived(*p))
     after_wave(1)
     wave(2)
@@ -321,16 +316,16 @@
     sums = (zero,) * MOMENTS
     middle = low + RING // 2
     for side, start, stop in (
+        (1, lambda d: high - d, lambda d: last - d),
         (0, lambda d: d + 1, lambda d: low + d),
-        (1, lambda d: high - d, lambda d: last - d),
     ):
         blocks = field.at[pl.ds(1, 3) if side == 0 else pl.ds(high, HALO)]
         some_copies(blocks, HALO_BLOCK, halo_recv.at[side]).wait_recv()
         planes(field, v0, 0.0, start(1), stop(1))
         planes(v0, v1, SHIFT, start(2), stop(2))
         planes(v1, v2, SHIFT, start(3), stop(3))
-        if side == 0:
-            sums = lax.fori_loop(low, middle, moments, sums, unroll=2)
+        if side == 1:
+            sums = lax.fori_loop(middle, high, moments, sums, unroll=True)
 
     for chip, c in outside + [partner]:
         number = 2 * chip + c
@@ -343,7 +338,7 @@
                 in_ring(chip, c),
             )
 
-    sums = lax.fori_loop(middle, high, moments, sums, unroll=2)
+    sums = lax.fori_loop(low, middle, moments, sums, unroll=True)
 
     far = sorted(
         ((dy, dz) for dy in range(count_y) for dz in range(count_z) if (dy, dz) != (0, 0)),
@@ -432,19 +427,17 @@
             recv_sem.at[FACTORS],
             in_ring(chip, c),
         )
-    for chip, c in outside + [partner]:
-        number = 2 * chip + c
-        issue(
-            u_send.at[layer(number, x)],
-            u_home.at[place, late],
-            LATE_ROWS,
-            recv_sem.at[LATE_ROWS],
-            in_ring(chip, c),
-        )
-    early = pl.ds(0, EARLY)
-    mine = layer(place, x)
-    u_home[place, late] = u_send[mine]
-    u_home[place, early] = combined(mine, early)
+    def send_u(*devices):
+        for chip, c in devices:
+            issue(
+                u_send.at[layer(2 * chip + c, x)],
+                u_home.at[place, late],
+                LATE_ROWS,
+                recv_sem.at[LATE_ROWS],
+                in_ring(chip, c),
+            )
+
+    send_u((across, core), (across, 1 - core))
 
     g = entries(total(1, groups), MOMENTS)
     own = (
@@ -465,6 +458,13 @@
         remote(
             own_rows.at[2], rows.at[2, place], row_sent.at[2], row_recv.at[2], in_ring(*p)
         ).start()
+
+    send_u((right, core), (left, core), partner, (right, 1 - core), (left, 1 - core))
+    early = pl.ds(0, EARLY)
+    mine = layer(place, x)
+    u_home[place, late] = u_send[mine]
+    u_home[place, early] = combined(mine, early)
+
 
     all_copies(EARLY_ROWS).wait_recv()
     all_copies(FACTORS).wait_recv()

time: 37.2 us -> 36.7 us (0.987)
  Pallas kernels: 36.5 us -> 36 us
    pallas_call x1, Pallas kernels: 35.7 us -> 35.2 us  [shards(): pl.pallas_call(functools.partial(kernel, sizes, cells), out_shape=(jax.Sh...]
where the time goes in v5:
time: 36.7 us; the launch traced here: 36.6 us
  Pallas kernels  36 us (98%)
  between operations  0.64 us (2%)
    pallas_call x1, Pallas kernels, shards(): pl.pallas_call(functools.partial(kernel, sizes, cells), out_shape=(jax.Sh...  35.2 us
    pallas_call x1, Pallas kernels, shards(): pl.pallas_call(deliver, out_shape=(jax.ShapeDtypeStruct(u.shape, f32), ja...  0.81 us

profile of v5, /device:TPU:1, one launch (start us, length us, event | category | flops | bytes accessed | tf_op | source)
XLA Modules:
  0.0 36.6 jit_solution(15765092437054184088)
XLA Ops:
  0.6 35.2 %section.1 = (f32[8,64,256]{2,1,0:T(8,128)S(1)}, f32[8,128]{1,0:T(8,128)S(1)}) custom-call(f32[8,1,64,256]{3,2,1,0:T(8,128)} %state.1, f32[2,8,1,64,256]{4,3,2,1,0:T(8,128)} %explicit.1, f32[2,8,1,64,256]{4,3,2,1,0:T(8,128)} %implicit.1, f32[8]{0:T(128)} %coef.1), custom_call_target="tpu_custom_call" | custom-call | tf_op jit(solution)/shard_map/section/pallas_call | solution.py:510
  35.8 0.8 %deliver.1 = (f32[8,64,256]{2,1,0:T(8,128)}, f32[1,1]{1,0:T(1,128)}) custom-call(f32[8,64,256]{2,1,0:T(8,128)S(1)} %get-tuple-element.6.u, f32[8,128]{1,0:T(8,128)S(1)} %get-tuple-element.7.rms), custom_call_target="tpu_custom_call" | custom-call | tf_op jit(solution)/shard_map/deliver/pallas_call | solution.py:554

commit v6 on v5

--- a/solution.py
+++ b/solution.py
@@ -437,7 +437,7 @@
                 in_ring(chip, c),
             )
 
-    send_u((across, core), (across, 1 - core))
+    send_u((across, core), (right, core), (left, core), (across, 1 - core))
 
     g = entries(total(1, groups), MOMENTS)
     own = (
@@ -459,7 +459,7 @@
             own_rows.at[2], rows.at[2, place], row_sent.at[2], row_recv.at[2], in_ring(*p)
         ).start()
 
-    send_u((right, core), (left, core), partner, (right, 1 - core), (left, 1 - core))
+    send_u(partner, (right, 1 - core), (left, 1 - core))
     early = pl.ds(0, EARLY)
     mine = layer(place, x)
     u_home[place, late] = u_send[mine]

time: 36.7 us -> 36.4 us (level)
  Pallas kernels: 36 us -> 35.6 us
where the time goes in v6:
time: 36.4 us; the launch traced here: 36.3 us
  Pallas kernels  35.6 us (98%)
  between operations  0.64 us (2%)
    pallas_call x1, Pallas kernels, shards(): pl.pallas_call(functools.partial(kernel, sizes, cells), out_shape=(jax.Sh...  34.8 us
    pallas_call x1, Pallas kernels, shards(): pl.pallas_call(deliver, out_shape=(jax.ShapeDtypeStruct(u.shape, f32), ja...  0.81 us

profile of v6, /device:TPU:1, one launch (start us, length us, event | category | flops | bytes accessed | tf_op | source)
XLA Modules:
  0.0 36.3 jit_solution(748888146145781065)
XLA Ops:
  0.6 34.8 %section.1 = (f32[8,64,256]{2,1,0:T(8,128)S(1)}, f32[8,128]{1,0:T(8,128)S(1)}) custom-call(f32[8,1,64,256]{3,2,1,0:T(8,128)} %state.1, f32[2,8,1,64,256]{4,3,2,1,0:T(8,128)} %explicit.1, f32[2,8,1,64,256]{4,3,2,1,0:T(8,128)} %implicit.1, f32[8]{0:T(128)} %coef.1), custom_call_target="tpu_custom_call" | custom-call | tf_op jit(solution)/shard_map/section/pallas_call | solution.py:510
  35.5 0.8 %deliver.1 = (f32[8,64,256]{2,1,0:T(8,128)}, f32[1,1]{1,0:T(1,128)}) custom-call(f32[8,64,256]{2,1,0:T(8,128)S(1)} %get-tuple-element.6.u, f32[8,128]{1,0:T(8,128)S(1)} %get-tuple-element.7.rms), custom_call_target="tpu_custom_call" | custom-call | tf_op jit(solution)/shard_map/deliver/pallas_call | solution.py:554

commit v7 on v6

--- a/solution.py
+++ b/solution.py
@@ -459,7 +459,7 @@
             own_rows.at[2], rows.at[2, place], row_sent.at[2], row_recv.at[2], in_ring(*p)
         ).start()
 
-    send_u(partner, (right, 1 - core), (left, 1 - core))
+    send_u((right, 1 - core), (left, 1 - core), partner)
     early = pl.ds(0, EARLY)
     mine = layer(place, x)
     u_home[place, late] = u_send[mine]

time: 36.4 us -> 36.4 us (level)
  no operation moved by 1% of the time
where the time goes in v7:
time: 36.4 us; the launch traced here: 36.3 us
  Pallas kernels  35.6 us (98%)
  between operations  0.64 us (2%)
    pallas_call x1, Pallas kernels, shards(): pl.pallas_call(functools.partial(kernel, sizes, cells), out_shape=(jax.Sh...  34.8 us
    pallas_call x1, Pallas kernels, shards(): pl.pallas_call(deliver, out_shape=(jax.ShapeDtypeStruct(u.shape, f32), ja...  0.81 us

profile of v7, /device:TPU:1, one launch (start us, length us, event | category | flops | bytes accessed | tf_op | source)
XLA Modules:
  0.0 36.3 jit_solution(15448053627905683079)
XLA Ops:
  0.6 34.8 %section.1 = (f32[8,64,256]{2,1,0:T(8,128)S(1)}, f32[8,128]{1,0:T(8,128)S(1)}) custom-call(f32[8,1,64,256]{3,2,1,0:T(8,128)} %state.1, f32[2,8,1,64,256]{4,3,2,1,0:T(8,128)} %explicit.1, f32[2,8,1,64,256]{4,3,2,1,0:T(8,128)} %implicit.1, f32[8]{0:T(128)} %coef.1), custom_call_target="tpu_custom_call" | custom-call | tf_op jit(solution)/shard_map/section/pallas_call | solution.py:510
  35.5 0.8 %deliver.1 = (f32[8,64,256]{2,1,0:T(8,128)}, f32[1,1]{1,0:T(1,128)}) custom-call(f32[8,64,256]{2,1,0:T(8,128)S(1)} %get-tuple-element.6.u, f32[8,128]{1,0:T(8,128)S(1)} %get-tuple-element.7.rms), custom_call_target="tpu_custom_call" | custom-call | tf_op jit(solution)/shard_map/deliver/pallas_call | solution.py:554
